TPU v7x, 32 devices: a whole 2x2x4 slice. The times are simulated.
32 devices in a mesh: head: 4 (over z), pts: 8 (over y, x, core).
Axes of the slice: x: 2, y: 2, z: 4, core: 2. Of those that a mesh axis runs over, the one named last changes fastest.
Arguments:
- layer_inputs_trainorder: bfloat16 [196608, 256], P(('head', 'pts')), may hold values from -6 to 6
- inference_placement: int32 [196608], P(('head', 'pts')), may hold values from 0 to 196607, as said below
- initial_layernorm_gain: float32 [256], replicated, may hold values from 0.1 to 1.9
- initial_layernorm_offset: float32 [256], replicated, may hold values from -2 to 2
- attribute_projection: bfloat16 [256, 256], replicated, may hold values from -0.375 to 0.375
- assignment_feeder_projection: bfloat16 [256, 256], replicated, may hold values from -0.375 to 0.375
- partition_projection: bfloat16 [16, 32], replicated, may hold values from -1.5 to 1.5
- partition_offset: float32 [32], replicated, may hold values from -4 to 4
- softmax_sharpness: float32 [16], P('head'), may hold values from 0.03 to 1
- partition_question_map: float32 [16, 16], replicated, may hold values from -1.5 to 1.5
- partition_lookup_map: float32 [16, 16], replicated, may hold values from -1.5 to 1.5
- partition_content_map: float32 [16, 16], replicated, may hold values from -1.5 to 1.5
- emitted_projection: bfloat16 [256, 256], replicated, may hold values from -0.375 to 0.375
- emitted_offset: float32 [256], replicated, may hold values from -2 to 2
- latter_layernorm_gain: float32 [256], replicated, may hold values from 0.1 to 1.9
- latter_layernorm_offset: float32 [256], replicated, may hold values from -2 to 2
- perceptron_entry_map: bfloat16 [256, 1024], replicated, may hold values from -0.375 to 0.375
- perceptron_entry_offset: float32 [1024], replicated, may hold values from -2 to 2
- perceptron_exit_map: bfloat16 [1024, 256], replicated, may hold values from -0.1875 to 0.1875
- perceptron_exit_offset: float32 [256], replicated, may hold values from -2 to 2
Outputs:
- served: bfloat16 [8, 24576, 256], P('pts', 'head')
Inputs may be any that keep to these rules, and one draw needn't show every extreme that they name: inference_placement is a permutation of all points; of the 6144 points of each aligned block of the training order, exactly 192 go to each aligned block of 6144 serving positions.
All inputs are finite; a program needn't handle non-finite values.
Results may differ from a plain program's by a relative error of at most 0.0035.
The roundings to bfloat16 on the way count: a program that leaves them out, or rounds other values in their place, can miss the bound.
Values may be sent and summed in bfloat16 or wider, within the bound.
A program may use at most 128 MiB of HBM per device.

v0:
```python
import math

import jax
import jax.numpy as jnp
from jax import lax
from jax.sharding import PartitionSpec as P

DH = 16


def layer_norm(row_block, gain_vec, bias_vec):
    row_mean = jnp.mean(row_block, axis=-1, keepdims=True)
    centred = row_block - row_mean
    spread = jnp.mean(centred * centred, axis=-1, keepdims=True)
    return centred * lax.rsqrt(spread + 1e-05) * gain_vec + bias_vec


def move_rows(rows, labels, ordering):
    arrived = lax.all_to_all(
        rows[ordering], ("head", "pts"), split_axis=0, concat_axis=0, tiled=True
    )
    arrived_labels = lax.all_to_all(
        labels, ("head", "pts"), split_axis=0, concat_axis=0, tiled=True
    )
    placed = jnp.argsort(arrived_labels[:, 0])
    return (arrived[placed], arrived_labels[placed, 1])


def slice_attention(
    totals, numerator, partition_question_map, partition_lookup_map, partition_content_map
):
    slice_token = numerator / (totals + 1e-05)[:, :, None]
    highest_mode = lax.Precision.HIGHEST
    query_rows = jnp.einsum(
        "izn,nu->izu", slice_token, partition_question_map, precision=highest_mode
    )
    key_vectors = jnp.einsum(
        "izn,nu->izu", slice_token, partition_lookup_map, precision=highest_mode
    )
    value_rows = jnp.einsum(
        "izn,nu->izu", slice_token, partition_content_map, precision=highest_mode
    )
    score_scale = 1.0 / math.sqrt(DH)
    scores = (
        jnp.einsum("hme,hne->hmn", query_rows, key_vectors, precision=highest_mode) * score_scale
    )
    attention = jax.nn.softmax(scores, axis=-1)
    return jnp.einsum("hmn,hne->hme", attention, value_rows, precision=highest_mode).astype(
        jnp.bfloat16
    )


def finish_rows(
    residual_rows,
    blended_rows,
    emitted_projection,
    emitted_offset,
    latter_layernorm_gain,
    latter_layernorm_offset,
    perceptron_entry_map,
    perceptron_entry_offset,
    perceptron_exit_map,
    perceptron_exit_offset,
):
    hidden = (
        residual_rows.astype(jnp.float32)
        + jnp.dot(blended_rows, emitted_projection, preferred_element_type=jnp.float32)
        + emitted_offset
    )
    normed_two = layer_norm(hidden, latter_layernorm_gain, latter_layernorm_offset).astype(
        jnp.bfloat16
    )
    inner_act = jax.nn.gelu(
        jnp.dot(normed_two, perceptron_entry_map, preferred_element_type=jnp.float32)
        + perceptron_entry_offset,
        approximate=False,
    ).astype(jnp.bfloat16)
    return (
        hidden
        + jnp.dot(inner_act, perceptron_exit_map, preferred_element_type=jnp.float32)
        + perceptron_exit_offset
    ).astype(jnp.bfloat16)


def body(
    layer_inputs_trainorder,
    inference_placement,
    initial_layernorm_gain,
    initial_layernorm_offset,
    attribute_projection,
    assignment_feeder_projection,
    partition_projection,
    partition_offset,
    softmax_sharpness,
    partition_question_map,
    partition_lookup_map,
    partition_content_map,
    emitted_projection,
    emitted_offset,
    latter_layernorm_gain,
    latter_layernorm_offset,
    perceptron_entry_map,
    perceptron_entry_offset,
    perceptron_exit_map,
    perceptron_exit_offset,
):
    groups = lax.axis_size("head")
    shards = lax.axis_size("pts")
    local_rows = layer_inputs_trainorder.shape[0]
    model_width = layer_inputs_trainorder.shape[1]
    dest_block = inference_placement // local_rows
    target = dest_block % groups * shards + dest_block // groups
    ordering = jnp.argsort(target, stable=True)
    anchor = lax.axis_index(("head", "pts")) * local_rows + jnp.arange(local_rows, dtype=jnp.int32)
    labels = jnp.stack([inference_placement[ordering], anchor[ordering]], axis=1)
    sharpness_sequence = lax.all_gather(softmax_sharpness, "head", axis=0, tiled=True)
    every_attender = sharpness_sequence.shape[0]
    standardized_entries = layer_norm(
        layer_inputs_trainorder.astype(jnp.float32),
        initial_layernorm_gain,
        initial_layernorm_offset,
    ).astype(jnp.bfloat16)
    slice_feature_rows = (
        jnp.dot(standardized_entries, attribute_projection, preferred_element_type=jnp.float32)
        .astype(jnp.bfloat16)
        .reshape(local_rows, every_attender, DH)
    )
    middle = (
        jnp.dot(
            standardized_entries, assignment_feeder_projection, preferred_element_type=jnp.float32
        )
        .astype(jnp.bfloat16)
        .reshape(local_rows, every_attender, DH)
    )
    partition_scores_raw = jnp.einsum(
        "rhd,dm->rhm", middle, partition_projection, preferred_element_type=jnp.float32
    )
    partition_scores_raw = (partition_scores_raw + partition_offset) / sharpness_sequence[:, None]
    coefficient_array = jax.nn.softmax(partition_scores_raw, axis=-1)
    coefficients_halfprecision = coefficient_array.astype(jnp.bfloat16)
    totals = jnp.sum(coefficient_array, axis=0)
    numerator = jnp.einsum(
        "qct,qcv->ctv",
        coefficients_halfprecision,
        slice_feature_rows,
        preferred_element_type=jnp.float32,
    )
    totals, numerator = lax.psum((totals, numerator), ("head", "pts"))
    slice_output = slice_attention(
        totals, numerator, partition_question_map, partition_lookup_map, partition_content_map
    )
    blended_rows = (
        jnp.einsum(
            "fny,nyp->fnp",
            coefficients_halfprecision,
            slice_output,
            preferred_element_type=jnp.float32,
        )
        .astype(jnp.bfloat16)
        .reshape(local_rows, model_width)
    )
    result = finish_rows(
        layer_inputs_trainorder,
        blended_rows,
        emitted_projection,
        emitted_offset,
        latter_layernorm_gain,
        latter_layernorm_offset,
        perceptron_entry_map,
        perceptron_entry_offset,
        perceptron_exit_map,
        perceptron_exit_offset,
    )
    served, unused = move_rows(result, labels, ordering)
    return served[None]


def solution(mesh):
    placed = (
        P(("head", "pts"), None),
        P(("head", "pts")),
        P(),
        P(),
        P(),
        P(),
        P(),
        P(),
        P("head"),
        P(),
        P(),
        P(),
        P(),
        P(),
        P(),
        P(),
        P(),
        P(),
        P(),
        P(),
    )
    return jax.shard_map(
        body, mesh=mesh, in_specs=placed, out_specs=P("pts", "head", None), check_vma=False
    )
```

profile of v0, /device:TPU:0, one launch (start us, length us, event | category | flops | bytes accessed | tf_op | source)
XLA Modules:
  0.0 396.0 jit_solution(12887393150677298646)
XLA Ops:
  0.0 0.9 fusion.46
  0.9 6.7 %sort.34 = (s32[6144]{0:T(1024)}, s32[6144]{0:T(1024)S(1)}) sort(s32[6144]{0:T(1024)S(1)} %fusion.46, s32[6144]{0:T(1024)S(1)} %iota.11), dimensions={0}, to_apply=%region_11.12 | sort | flops 79872 | bytes 98304 | tf_op jit(solution)/shard_map/jit(argsort)/sort | solution.py:113
  7.7 34.3 %gather_fusion.1 = s32[6144]{0:T(1024)S(1)} fusion(s32[6144]{0:T(1024)S(1)} %copy-done.2, s32[6144]{0:T(1024)S(1)} %get-tuple-element.19), kind=kCustom, calls=%fused_computation.1 | custom fusion | bytes 73728 | tf_op jit(solution)/shard_map/gather | solution.py:115
  42.0 34.3 %gather_fusion.2 = s32[6144]{0:T(1024)S(1)} fusion(s32[6144]{0:T(1024)S(1)} %get-tuple-element.20, s32[6144]{0:T(1024)S(1)} %get-tuple-element.19), kind=kCustom, calls=%fused_computation.2 | custom fusion | bytes 73728 | tf_op jit(solution)/shard_map/gather | solution.py:115
  76.5 0.7 copy.42
  77.1 7.5 %all-to-all-start.1 = ((s32[32,192,2]{1,2,0:T(2,128)}), s32[32,192,2]{1,2,0:T(2,128)}, u32[]{:S(2)}, u32[]{:S(2)}) async-start(s32[32,192,2]{1,2,0:T(2,128)} %copy.42), calls=%async_computation.1 | async-start | bytes 131072 | tf_op jit(solution)/shard_map/all_to_all | solution.py:22
  84.6 4.6 %copy.35 = bf16[6144,256]{0,1:T(8,128)(2,1)} copy(bf16[6144,256]{1,0:T(8,128)(2,1)} %param.20) | data formatting | bytes 6291456 | tf_op args[0]
  89.2 2.4 convert_reduce_fusion
  91.7 2.7 fusion.27
  94.5 0.7 dynamic-slice
  96.1 12.0 %all-reduce = f32[16]{0:T(128)S(1)} all-reduce(f32[16]{0:T(128)S(1)} %dynamic-update-slice), channel_id=1, replica_groups=mesh['head'=4,'pts'=8] {'head'}, use_global_device_ids=true, to_apply=%add | all-reduce | flops 16 | bytes 128
  108.2 5.4 %convolution_convert_fusion.2 = bf16[6144,256]{0,1:T(8,128)(2,1)} fusion(bf16[256,256]{1,0:T(8,128)(2,1)S(1)} %copy-done.12, bf16[6144,256]{0,1:T(8,128)(2,1)} %copy.35, f32[256]{0:T(256)S(1)} %copy-done.19, f32[256]{0:T(256)S(1)} %copy-done.20, f32[6144]{0:T(1024)S(1)} %add_rsqrt_fusion.1, f32[6144]{0:T(1024)S(1)} %broadcast_multiply_fusion.1), kind=kOutput, calls=%fused_computation.36 | convolution fusion | flops 816316416 | bytes 6473728 | tf_op jit(solution)/shard_map/dot_general | solution.py:129
  113.6 3.4 convolution_convert_fusion.1
  117.0 10.9 %fusion.93 = (f32[6144,16]{0,1:T(8,128)S(1)}, f32[6144,16,32]{0,2,1:T(8,128)}) fusion(bf16[6144,16,16]{0,2,1:T(8,128)(2,1)} %bitcast.49, f32[16]{0:T(128)S(1)} %all-reduce, f32[32]{0:T(128)S(1)} %copy-done.25, bf16[16,32]{1,0:T(8,128)(2,1)S(1)} %copy-done.17), kind=kOutput, calls=%fused_computation.125 | convolution fusion | flops 113246240 | bytes 16123072 | tf_op jit(solution)/shard_map/sub | solution.py:139
  127.9 9.1 %fusion.31 = (f32[16,32]{1,0:T(8,128)S(1)}, bf16[6144,16,32]{0,2,1:T(8,128)(2,1)}) fusion(f32[6144,16,32]{0,2,1:T(8,128)} %get-tuple-element.14, f32[6144,16]{0,1:T(8,128)S(1)} %get-tuple-element.13), kind=kLoop, calls=%fused_computation.47 | loop fusion | flops 9436672 | bytes 19269632 | tf_op jit(solution)/shard_map/reduce_sum | solution.py:141
  137.0 4.6 %fusion.98 = f32[16,32,16]{1,2,0:T(8,128)S(1)} fusion(bf16[6144,16,32]{0,2,1:T(8,128)(2,1)} %get-tuple-element.12, bf16[6144,16,16]{0,2,1:T(8,128)(2,1)S(1)} %bitcast.47), kind=kOutput, calls=%fused_computation.128 | convolution fusion | flops 100663296 | bytes 9469952 | tf_op jit(solution)/shard_map/qct,qcv->ctv/dot_general | solution.py:142
  141.6 40.3 %all-reduce.1 = (f32[16,32,16]{1,2,0:T(8,128)S(1)}, f32[16,32]{1,0:T(8,128)S(1)}) all-reduce(f32[16,32,16]{1,2,0:T(8,128)S(1)} %fusion.98, f32[16,32]{1,0:T(8,128)S(1)} %get-tuple-element.11), channel_id=1, replica_groups=mesh['head'=4,'pts'=8] {'head','pts'}, use_global_device_ids=true, to_apply=%region_4.5 | all-reduce | flops 8704 | bytes 69632 | tf_op jit(solution)/shard_map/psum | solution.py:148
  182.9 0.6 fusion.94
  183.6 0.4 convolution_convert_fusion.3
  184.0 3.8 convolution_convert_fusion
  187.8 1.4 fusion.95
  189.2 0.7 multiply_reduce_fusion
  190.0 1.9 copy-done.5
  191.9 58.3 %fusion.119 = bf16[6144,1024]{1,0:T(8,128)(2,1)} fusion(f32[1024]{0:T(1024)S(1)} %copy-done.18, bf16[256,1024]{1,0:T(8,128)(2,1)S(1)} %copy-done, f32[6144,256]{0,1:T(8,128)S(1)} %get-tuple-element.18, f32[256]{0:T(256)S(1)} %copy-done.21, f32[256]{0:T(256)S(1)} %copy-done.22, f32[6144]{0:T(1024)S(1)} %add_rsqrt_fusion, ...), kind=kOutput, calls=%fused_computation.8.clone.clone.clone.clone.clone.clone.clone.clone.1 | convolution fusion | flops 3644325888 | bytes 19453952 | tf_op jit(solution)/shard_map/dot_general | solution.py:74
  250.2 15.5 %fusion.22 = bf16[6144,256]{0,1:T(8,128)(2,1)} fusion(f32[6144,256]{0,1:T(8,128)} %copy-done.5, bf16[1024,256]{1,0:T(8,128)(2,1)S(1)} %copy-done.11, f32[256]{0:T(256)S(1)} %copy-done.23, bf16[6144,1024]{1,0:T(8,128)(2,1)} %fusion.119), kind=kOutput, calls=%fused_computation.37 | convolution fusion | flops 3225944064 | bytes 22545408 | tf_op jit(solution)/shard_map/dot_general | solution.py:80
  265.7 3.2 copy.41
  268.9 25.1 %gather_fusion = bf16[6144,256]{1,0:T(8,128)(2,1)} fusion(bf16[6144,256]{1,0:T(8,128)(2,1)S(1)} %copy.41, s32[6144]{0:T(1024)S(1)} %copy-done.8), kind=kCustom, calls=%fused_computation | custom fusion | bytes 6316032 | tf_op jit(solution)/shard_map/gather | solution.py:20
  294.0 4.4 %all-to-all-start = ((bf16[32,192,256]{2,1,0:T(8,128)(2,1)}), bf16[32,192,256]{2,1,0:T(8,128)(2,1)}, u32[]{:S(2)}, u32[]{:S(2)}) async-start(bf16[32,192,256]{2,1,0:T(8,128)(2,1)} %bitcast.46), calls=%async_computation | async-start | bytes 6291456 | tf_op jit(solution)/shard_map/all_to_all | solution.py:19
  298.4 0.8 copy.43
  299.4 6.7 %sort.35 = (s32[6144]{0:T(1024)}, s32[6144]{0:T(1024)S(1)}) sort(s32[6144]{0:T(1024)S(1)} %bitcast.48, s32[6144]{0:T(1024)S(1)} %iota.13), dimensions={0}, to_apply=%region_12.13 | sort | flops 79872 | bytes 98304 | tf_op jit(solution)/shard_map/jit(argsort)/sort | solution.py:25
  306.1 63.6 %all-to-all-done = bf16[32,192,256]{2,1,0:T(8,128)(2,1)} async-done(((bf16[32,192,256]{2,1,0:T(8,128)(2,1)}), bf16[32,192,256]{2,1,0:T(8,128)(2,1)}, u32[]{:S(2)}, u32[]{:S(2)}) %all-to-all-start) | async-done | bytes 3145760 | tf_op jit(solution)/shard_map/all_to_all | solution.py:19
  369.7 25.9 %gather_fusion.3 = bf16[6144,256]{1,0:T(8,128)(2,1)} fusion(bf16[6144,256]{1,0:T(8,128)(2,1)} %bitcast.10, s32[6144]{0:T(1024)S(1)} %fusion.48), kind=kCustom, calls=%fused_computation.3 | custom fusion | bytes 6316032 | tf_op jit(solution)/shard_map/gather | solution.py:26
  (74 shorter events, 1.7 us)
Async XLA Ops:
  0.0 191.8 %copy-start = (bf16[256,1024]{1,0:T(8,128)(2,1)S(1)}, bf16[256,1024]{1,0:T(8,128)(2,1)}, u32[]{:S(2)}) copy-start(bf16[256,1024]{1,0:T(8,128)(2,1)} %param.36) | copy-start | bytes 1572868
  0.0 7.6 %copy-start.2 = (s32[6144]{0:T(1024)S(1)}, s32[6144]{0:T(1024)}, u32[]{:S(2)}) copy-start(s32[6144]{0:T(1024)} %param.21) | copy-start | bytes 73732
  7.6 34.3 %copy-start.7 = (s32[6144]{0:T(1024)}, s32[6144]{0:T(1024)S(1)}, u32[]{:S(2)}) copy-start(s32[6144]{0:T(1024)S(1)} %get-tuple-element.19) | copy-start | bytes 73732
  76.2 18.2 %copy-start.26 = (u32[32]{0:T(128)S(1)}, u32[32]{0:T(128)}, u32[]{:S(2)}) copy-start(u32[32]{0:T(128)} %constant.125) | copy-start | bytes 388
  76.3 19.6 %copy-start.24 = (f32[4]{0:T(128)S(1)}, f32[4]{0:T(128)}, u32[]{:S(2)}) copy-start(f32[4]{0:T(128)} %param.28) | copy-start | bytes 52
  76.3 31.9 %copy-start.12 = (bf16[256,256]{1,0:T(8,128)(2,1)S(1)}, bf16[256,256]{1,0:T(8,128)(2,1)}, u32[]{:S(2)}) copy-start(bf16[256,256]{1,0:T(8,128)(2,1)} %param.25) | copy-start | bytes 393220
  76.3 31.9 %copy-start.19 = (f32[256]{0:T(256)S(1)}, f32[256]{0:T(256)}, u32[]{:S(2)}) copy-start(f32[256]{0:T(256)} %param.23) | copy-start | bytes 3076
  76.3 31.9 %copy-start.20 = (f32[256]{0:T(256)S(1)}, f32[256]{0:T(256)}, u32[]{:S(2)}) copy-start(f32[256]{0:T(256)} %param.22) | copy-start | bytes 3076
  77.1 216.9 %all-to-all-start.1 = ((s32[32,192,2]{1,2,0:T(2,128)}), s32[32,192,2]{1,2,0:T(2,128)}, u32[]{:S(2)}, u32[]{:S(2)}) async-start(s32[32,192,2]{1,2,0:T(2,128)} %copy.42), calls=%async_computation.1 | async-start | bytes 131072 | tf_op jit(solution)/shard_map/all_to_all | solution.py:22
  89.2 24.4 %copy-start.13 = (bf16[256,256]{1,0:T(8,128)(2,1)S(1)}, bf16[256,256]{1,0:T(8,128)(2,1)}, u32[]{:S(2)}) copy-start(bf16[256,256]{1,0:T(8,128)(2,1)} %param.24) | copy-start | bytes 393220
  108.2 5.5 %copy-start.3 = (bf16[6144,256]{0,1:T(8,128)(2,1)S(1)}, bf16[6144,256]{0,1:T(8,128)(2,1)}, u32[]{:S(2)}) copy-start(bf16[6144,256]{0,1:T(8,128)(2,1)} %copy.35) | copy-start | bytes 9437188
  108.2 8.9 %copy-start.17 = (bf16[16,32]{1,0:T(8,128)(2,1)S(1)}, bf16[16,32]{1,0:T(8,128)(2,1)}, u32[]{:S(2)}) copy-start(bf16[16,32]{1,0:T(8,128)(2,1)} %param.26) | copy-start | bytes 3076
  108.2 8.9 %copy-start.25 = (f32[32]{0:T(128)S(1)}, f32[32]{0:T(128)}, u32[]{:S(2)}) copy-start(f32[32]{0:T(128)} %param.27) | copy-start | bytes 388
  127.9 9.1 %copy-start.6 = (bf16[6144,256]{0,1:T(8,128)(2,1)S(1)}, bf16[6144,256]{0,1:T(8,128)(2,1)}, u32[]{:S(2)}) copy-start(bf16[6144,256]{0,1:T(8,128)(2,1)} %convolution_convert_fusion.1) | copy-start | bytes 9437188
  127.9 54.0 %copy-start.14 = (f32[16,16]{1,0:T(8,128)S(1)}, f32[16,16]{1,0:T(8,128)}, u32[]{:S(2)}) copy-start(f32[16,16]{1,0:T(8,128)} %param.30) | copy-start | bytes 3076
  127.9 54.3 %copy-start.15 = (f32[16,16]{1,0:T(8,128)S(1)}, f32[16,16]{1,0:T(8,128)}, u32[]{:S(2)}) copy-start(f32[16,16]{1,0:T(8,128)} %param.29) | copy-start | bytes 3076
  127.9 54.6 %copy-start.16 = (f32[16,16]{1,0:T(8,128)S(1)}, f32[16,16]{1,0:T(8,128)}, u32[]{:S(2)}) copy-start(f32[16,16]{1,0:T(8,128)} %param.31) | copy-start | bytes 3076
  137.0 50.8 %copy-start.9 = (bf16[256,256]{1,0:T(8,128)(2,1)S(1)}, bf16[256,256]{1,0:T(8,128)(2,1)}, u32[]{:S(2)}) copy-start(bf16[256,256]{1,0:T(8,128)(2,1)} %param.32) | copy-start | bytes 393220
  137.0 50.8 %copy-start.10 = (f32[256]{0:T(256)S(1)}, f32[256]{0:T(256)}, u32[]{:S(2)}) copy-start(f32[256]{0:T(256)} %param.33) | copy-start | bytes 3076
  181.9 5.9 %copy-start.4 = (bf16[6144,256]{0,1:T(8,128)(2,1)S(1)}, bf16[6144,256]{0,1:T(8,128)(2,1)}, u32[]{:S(2)}) copy-start(bf16[6144,256]{0,1:T(8,128)(2,1)} %copy.35) | copy-start | bytes 9437188
  187.7 4.1 %copy-start.18 = (f32[1024]{0:T(1024)S(1)}, f32[1024]{0:T(1024)}, u32[]{:S(2)}) copy-start(f32[1024]{0:T(1024)} %param.37) | copy-start | bytes 12292
  187.7 4.1 %copy-start.21 = (f32[256]{0:T(256)S(1)}, f32[256]{0:T(256)}, u32[]{:S(2)}) copy-start(f32[256]{0:T(256)} %param.35) | copy-start | bytes 3076
  187.8 4.1 %copy-start.22 = (f32[256]{0:T(256)S(1)}, f32[256]{0:T(256)}, u32[]{:S(2)}) copy-start(f32[256]{0:T(256)} %param.34) | copy-start | bytes 3076
  189.2 2.6 copy-start.5
  191.8 58.4 %copy-start.11 = (bf16[1024,256]{1,0:T(8,128)(2,1)S(1)}, bf16[1024,256]{1,0:T(8,128)(2,1)}, u32[]{:S(2)}) copy-start(bf16[1024,256]{1,0:T(8,128)(2,1)} %param.38) | copy-start | bytes 1572868
  191.9 58.3 %copy-start.23 = (f32[256]{0:T(256)S(1)}, f32[256]{0:T(256)}, u32[]{:S(2)}) copy-start(f32[256]{0:T(256)} %param.39) | copy-start | bytes 3076
  250.2 18.7 %copy-start.8 = (s32[6144]{0:T(1024)S(1)}, s32[6144]{0:T(1024)}, u32[]{:S(2)}) copy-start(s32[6144]{0:T(1024)} %copy-done.7) | copy-start | bytes 73732
  294.0 75.7 %all-to-all-start = ((bf16[32,192,256]{2,1,0:T(8,128)(2,1)}), bf16[32,192,256]{2,1,0:T(8,128)(2,1)}, u32[]{:S(2)}, u32[]{:S(2)}) async-start(bf16[32,192,256]{2,1,0:T(8,128)(2,1)} %bitcast.46), calls=%async_computation | async-start | bytes 6291456 | tf_op jit(solution)/shard_map/all_to_all | solution.py:19
  369.7 25.9 %copy-start.1 = (bf16[256,1024]{1,0:T(8,128)(2,1)S(1)}, bf16[256,1024]{1,0:T(8,128)(2,1)}, u32[]{:S(2)}) copy-start(bf16[256,1024]{1,0:T(8,128)(2,1)} %param.36) | copy-start | bytes 1572868
where the time goes:
time: 402 us; the launch traced here: 396 us
  local copies, waits for them, and re-layouts  132 us (33%)
  matrix products  105 us (26%)
  waiting for transfers between devices  63.6 us (16%)
  blocking collectives  52.3 us (13%)
  other arithmetic  29.4 us (7%)
  starting transfers between devices  11.8 us (3%)
    all_to_all x1, waiting for transfers between devices, move_rows(): lax.all_to_all(rows[ordering], ('head', 'pts'), split_axis=0, concat_axis...  63.6 us
    dot_general x1, matrix products, finish_rows(): jnp.dot(normed_two, perceptron_entry_map, preferred_element_type=jnp.floa...  58.3 us
    psum x1, blocking collectives, body(): totals, numerator = lax.psum((totals, numerator), ('head', 'pts'))  40.3 us
    gather x1, local copies, waits for them, and re-layouts, body(): inference_placement[ordering]  34.3 us
    gather x1, local copies, waits for them, and re-layouts, body(): anchor[ordering]  34.3 us
    gather x1, local copies, waits for them, and re-layouts, move_rows(): return (arrived[placed], arrived_labels[placed, 1])  25.9 us
    gather x1, local copies, waits for them, and re-layouts, move_rows(): rows[ordering]  25.1 us
    dot_general x1, matrix products, finish_rows(): jnp.dot(inner_act, perceptron_exit_map, preferred_element_type=jnp.float32)  15.5 us
  transfers between devices with their start and end apart: 2, of which 1 were waited for; matrix products, arithmetic and copies ran while one was open for 41% of the time, Pallas kernels for 0%

commit v1 on v0

v1 whole, which is shorter than its diff:
```python
import functools
import math

import jax
import jax.numpy as jnp
from jax import lax
from jax.experimental import pallas as pl
from jax.experimental.pallas import tpu as pltpu
from jax.sharding import PartitionSpec as P

DH = 16
TILE = 512
F32 = jnp.float32
BF16 = jnp.bfloat16
HIGHEST = lax.Precision.HIGHEST
LOG2E = math.log2(math.e)
NT = (((1,), (1,)), ((), ()))


def norm_rows(rows, gain, bias):
    mean = jnp.mean(rows, axis=-1, keepdims=True)
    centred = rows - mean
    spread = jnp.mean(centred * centred, axis=-1, keepdims=True)
    return (centred * lax.rsqrt(spread + 1e-05) * gain + bias).astype(BF16)


def slice_weights(feeder_t, expand, offset, scale, slices):
    raw = jnp.dot(expand, feeder_t, preferred_element_type=F32)
    logit = (raw + offset) * scale
    lanes = logit.shape[1]
    logit = logit.reshape(-1, slices, lanes)
    powers = jnp.exp2(logit - jnp.max(logit, axis=1, keepdims=True))
    share = powers * (1.0 / jnp.sum(powers, axis=1, keepdims=True))
    return share.reshape(-1, lanes)


def same_head(shape, row_size, column_size):
    row_head = lax.broadcasted_iota(jnp.int32, shape, 0) // row_size
    column_head = lax.broadcasted_iota(jnp.int32, shape, 1) // column_size
    return row_head == column_head


def sums_kernel(
    slices, x_ref, gain_ref, bias_ref, w_ref, expand_ref, offset_ref, scale_ref,
    out_ref, numer, total,
):
    step = pl.program_id(0)
    width = x_ref.shape[1]

    @pl.when(step == 0)
    def _():
        numer[...] = jnp.zeros_like(numer)
        total[...] = jnp.zeros_like(total)

    normed = norm_rows(x_ref[...].astype(F32), gain_ref[...], bias_ref[...])
    both = lax.dot_general(w_ref[...], normed, NT, preferred_element_type=F32).astype(BF16)
    share = slice_weights(
        both[width:], expand_ref[...], offset_ref[...], scale_ref[...], slices
    )
    numer[...] += lax.dot_general(
        both[:width], share.astype(BF16), NT, preferred_element_type=F32
    )
    lanes = total.shape[1]
    part = share[:, :lanes]
    for at in range(lanes, share.shape[1], lanes):
        part += share[:, at : at + lanes]
    total[...] += part

    @pl.when(step == pl.num_programs(0) - 1)
    def _():
        kept = jnp.where(same_head(numer.shape, DH, slices), numer[...], 0.0)
        out_ref[:DH] = jnp.sum(kept.reshape(-1, DH, kept.shape[1]), axis=0)
        out_ref[DH:] = lax.dot_general(
            jnp.ones((8, lanes), F32), total[...], NT, precision=HIGHEST,
            preferred_element_type=F32,
        )


def exact_gelu(h):
    size = jnp.abs(h)
    t = 1.0 / (1.0 + (0.3275911 / math.sqrt(2.0)) * size)
    poly = (0.5 * 1.061405429) * t + (0.5 * -1.453152027)
    poly = poly * t + (0.5 * 1.421413741)
    poly = poly * t + (0.5 * -0.284496736)
    poly = poly * t + (0.5 * 0.254829592)
    tail = (poly * t) * jnp.exp2((h * h) * (-0.5 * LOG2E))
    return jnp.maximum(h, 0.0) - size * tail


def rows_kernel(
    slices, x_ref, sums_ref, qkv_ref, gain_ref, bias_ref, w_ref, expand_ref, offset_ref,
    scale_ref, emit_ref, emit_bias_ref, gain2_ref, bias2_ref, entry_ref, entry_bias_ref,
    exit_ref, exit_bias_ref, out_ref, blend,
):
    @pl.when(pl.program_id(0) == 0)
    def _():
        stok = sums_ref[:DH] / (sums_ref[DH : DH + 1] + 1e-05)
        qkv = jnp.dot(qkv_ref[...], stok, precision=HIGHEST, preferred_element_type=F32)
        query, key, value = qkv[:DH], qkv[DH : 2 * DH], qkv[2 * DH :]
        scores = jnp.dot(key.T, query, precision=HIGHEST, preferred_element_type=F32)
        scores = scores * (1.0 / math.sqrt(DH))
        mask = same_head(scores.shape, slices, slices)
        scores = jnp.where(mask, scores, -jnp.inf)
        powers = jnp.exp(scores - jnp.max(scores, axis=0, keepdims=True))
        attention = powers / jnp.sum(powers, axis=0, keepdims=True)
        sout = jnp.dot(value, attention, precision=HIGHEST, preferred_element_type=F32)
        spread = jnp.concatenate([sout] * (blend.shape[0] // DH), axis=0)
        blend[...] = jnp.where(same_head(blend.shape, DH, slices), spread, 0.0).astype(BF16)

    x = x_ref[...].astype(F32)
    normed = norm_rows(x, gain_ref[...], bias_ref[...])
    feeder = lax.dot_general(w_ref[...], normed, NT, preferred_element_type=F32).astype(BF16)
    share = slice_weights(feeder, expand_ref[...], offset_ref[...], scale_ref[...], slices)
    mixed = jnp.dot(blend[...], share.astype(BF16), preferred_element_type=F32)
    y = (
        x
        + jnp.dot(mixed.T.astype(BF16), emit_ref[...], preferred_element_type=F32)
        + emit_bias_ref[...]
    )
    z = norm_rows(y, gain2_ref[...], bias2_ref[...])
    result = y + exit_bias_ref[...]
    chunk = x_ref.shape[1]
    for at in range(0, entry_ref.shape[1], chunk):
        h = jnp.dot(z, entry_ref[:, at : at + chunk], preferred_element_type=F32)
        g = exact_gelu(h + entry_bias_ref[:, at : at + chunk]).astype(BF16)
        result += jnp.dot(g, exit_ref[at : at + chunk], preferred_element_type=F32)
    out_ref[...] = result.astype(BF16)


def whole(array):
    return pl.BlockSpec(array.shape, lambda i: (0,) * array.ndim)


def body(
    layer_inputs_trainorder,
    inference_placement,
    initial_layernorm_gain,
    initial_layernorm_offset,
    attribute_projection,
    assignment_feeder_projection,
    partition_projection,
    partition_offset,
    softmax_sharpness,
    partition_question_map,
    partition_lookup_map,
    partition_content_map,
    emitted_projection,
    emitted_offset,
    latter_layernorm_gain,
    latter_layernorm_offset,
    perceptron_entry_map,
    perceptron_entry_offset,
    perceptron_exit_map,
    perceptron_exit_offset,
):
    groups = lax.axis_size("head")
    shards = lax.axis_size("pts")
    devices = groups * shards
    local_rows, width = layer_inputs_trainorder.shape
    per_pair = local_rows // devices
    own_heads = softmax_sharpness.shape[0]
    heads = own_heads * groups
    slices = partition_projection.shape[1]
    columns = heads * slices
    tile = math.gcd(TILE, local_rows)

    dest_block = inference_placement // local_rows
    target = dest_block % groups * shards + dest_block // groups
    send_key = target * local_rows + inference_placement % local_rows
    counting = jnp.arange(local_rows, dtype=jnp.int32)
    send_key, ordering = lax.sort((send_key, counting), num_keys=1)
    spots = (send_key % local_rows).astype(F32).reshape(devices, per_pair)
    small = jnp.concatenate(
        [spots, jnp.broadcast_to(softmax_sharpness, (devices, own_heads))], axis=1
    )
    small = lax.all_to_all(small, ("head", "pts"), split_axis=0, concat_axis=0, tiled=True)
    sharpness = small.reshape(groups, shards, -1)[:, 0, per_pair:].reshape(heads)
    arrived_spots = small[:, :per_pair].reshape(local_rows).astype(jnp.int32)
    arrived = lax.all_to_all(
        layer_inputs_trainorder[ordering], ("head", "pts"), split_axis=0, concat_axis=0,
        tiled=True,
    )
    _, placed = lax.sort((arrived_spots, counting), num_keys=1)

    gain = initial_layernorm_gain[None]
    bias = initial_layernorm_offset[None]
    feeder_t = assignment_feeder_projection.T
    both_t = jnp.concatenate([attribute_projection.T, feeder_t], axis=0)
    expand = (
        jnp.eye(heads, dtype=BF16)[:, None, :, None] * partition_projection.T[None, :, None, :]
    ).reshape(columns, width)
    offset = jnp.tile(partition_offset, heads)[:, None]
    scale = jnp.repeat(LOG2E / sharpness, slices)[:, None]

    row_spec = pl.BlockSpec((tile, width), lambda i: (i, 0))
    operands = (gain, bias, both_t, expand, offset, scale)
    sums = pl.pallas_call(
        functools.partial(sums_kernel, slices),
        grid=(local_rows // tile,),
        in_specs=[row_spec] + [whole(a) for a in operands],
        out_specs=pl.BlockSpec((DH + 8, columns), lambda i: (0, 0)),
        out_shape=jax.ShapeDtypeStruct((DH + 8, columns), F32),
        scratch_shapes=[pltpu.VMEM((width, columns), F32), pltpu.VMEM((columns, 128), F32)],
        compiler_params=pltpu.CompilerParams(dimension_semantics=("arbitrary",)),
        cost_estimate=pl.CostEstimate(
            flops=local_rows * width * columns * 8, bytes_accessed=local_rows * width * 16,
            transcendentals=local_rows * columns,
        ),
    )(layer_inputs_trainorder, *operands)
    sums = lax.psum(sums, ("head", "pts"))

    qkv = jnp.concatenate(
        [partition_question_map.T, partition_lookup_map.T, partition_content_map.T], axis=0
    )
    operands = (
        sums, qkv, gain, bias, feeder_t, expand, offset, scale, emitted_projection,
        emitted_offset[None], latter_layernorm_gain[None], latter_layernorm_offset[None],
        perceptron_entry_map, perceptron_entry_offset[None], perceptron_exit_map,
        perceptron_exit_offset[None],
    )
    result = pl.pallas_call(
        functools.partial(rows_kernel, slices),
        grid=(local_rows // tile,),
        in_specs=[row_spec] + [whole(a) for a in operands],
        out_specs=row_spec,
        out_shape=jax.ShapeDtypeStruct((local_rows, width), BF16),
        scratch_shapes=[pltpu.VMEM((width, columns), BF16)],
        compiler_params=pltpu.CompilerParams(dimension_semantics=("arbitrary",)),
        cost_estimate=pl.CostEstimate(
            flops=local_rows * width * columns * 16, bytes_accessed=local_rows * width * 16,
            transcendentals=local_rows * columns * 4,
        ),
    )(arrived, *operands)
    return result[placed][None]


def solution(mesh):
    placed = (
        P(("head", "pts"), None),
        P(("head", "pts")),
        P(),
        P(),
        P(),
        P(),
        P(),
        P(),
        P("head"),
        P(),
        P(),
        P(),
        P(),
        P(),
        P(),
        P(),
        P(),
        P(),
        P(),
        P(),
    )
    return jax.shard_map(
        body, mesh=mesh, in_specs=placed, out_specs=P("pts", "head", None), check_vma=False
    )
```

time: 402 us -> 211 us (0.52); the launches traced: 396 us -> 210 us
  matrix products: 105 us -> 0 us
  local copies, waits for them, and re-layouts: 132 us -> 58.1 us
  waiting for transfers between devices: 63.6 us -> 0.01 us
  Pallas kernels: 0 us -> 62.1 us
  other arithmetic: 29.4 us -> 14.8 us
  blocking collectives: 52.3 us -> 61.7 us
    dot_general x12 -> x0, matrix products: 94.3 us -> none  [the longest x1 58.3 us: finish_rows(): jnp.dot(normed_two, perceptron_entry_map, preferred_element_type=jnp.floa...]
    gather x4 -> x2, local copies, waits for them, and re-layouts: 120 us -> 51.7 us  [the longest x1 25.8 us: body(): layer_inputs_trainorder[ordering]]
    all_to_all x2, waiting for transfers between devices: 63.6 us -> 0.01 us  [the longest x1 0.01 us: body(): lax.all_to_all(small, ('head', 'pts'), split_axis=0, concat_axis=0, tiled...]
    pallas_call x0 -> x2, Pallas kernels: none -> 62.1 us  [the longest x1 44.3 us: body(): pl.pallas_call(functools.partial(rows_kernel, slices), grid=(local_rows /...]
    psum x1, blocking collectives: 40.3 us -> 61.7 us  [body(): sums = lax.psum(sums, ('head', 'pts'))]
    reduce_sum x5 -> x0, other arithmetic: 15 us -> none  [the longest x1 9.07 us: body(): totals = jnp.sum(coefficient_array, axis=0)]
    unnamed x1 -> x0, blocking collectives: 12 us -> none
    sub x1 -> x0, matrix products: 10.9 us -> none  [body(): coefficient_array = jax.nn.softmax(partition_scores_raw, axis=-1)]
  transfers between devices with their start and end apart: 2 -> 2, of which waited for: 1 -> 0; matrix products, arithmetic and copies ran while one was open for 41% -> 18% of each run, Pallas kernels for 0% -> 8%
where the time goes in v1:
time: 211 us; the launch traced here: 210 us
  Pallas kernels  62.1 us (29%)
  blocking collectives  61.7 us (29%)
  local copies, waits for them, and re-layouts  58.1 us (28%)
  other arithmetic  14.8 us (7%)
  starting transfers between devices  13.3 us (6%)
    psum x1, blocking collectives, body(): sums = lax.psum(sums, ('head', 'pts'))  61.7 us
    pallas_call x1, Pallas kernels, body(): pl.pallas_call(functools.partial(rows_kernel, slices), grid=(local_rows /...  44.3 us
    gather x1, local copies, waits for them, and re-layouts, body(): layer_inputs_trainorder[ordering]  25.8 us
    gather x1, local copies, waits for them, and re-layouts, body(): return result[placed][None]  25.8 us
    pallas_call x1, Pallas kernels, body(): pl.pallas_call(functools.partial(sums_kernel, slices), grid=(local_rows /...  17.8 us
    all_to_all x1, starting transfers between devices, body(): lax.all_to_all(small, ('head', 'pts'), split_axis=0, concat_axis=0, tiled...  7.33 us
    sort x1, other arithmetic, body(): _, placed = lax.sort((arrived_spots, counting), num_keys=1)  6.73 us
    sort x1, other arithmetic, body(): send_key, ordering = lax.sort((send_key, counting), num_keys=1)  6.2 us
  transfers between devices with their start and end apart: 2, of which 0 were waited for; matrix products, arithmetic and copies ran while one was open for 18% of the time, Pallas kernels for 8%

profile of v1, /device:TPU:0, one launch (start us, length us, event | category | flops | bytes accessed | tf_op | source)
XLA Modules:
  0.0 210.2 jit_solution(14148470757854736010)
XLA Ops:
  0.0 0.8 fusion.3
  0.8 6.2 %sort.30 = (s32[6144]{0:T(1024)S(1)}, s32[6144]{0:T(1024)S(1)}) sort(s32[6144]{0:T(1024)S(1)} %fusion.3, s32[6144]{0:T(1024)S(1)} %iota.19), dimensions={0}, to_apply=%region_0.1 | sort | flops 79872 | bytes 98304 | tf_op jit(solution)/shard_map/sort | solution.py:171
  7.0 0.1 reshape.29
  7.1 0.7 pad.4.clone
  7.9 0.6 all_to_all.18
  8.5 7.3 %all-to-all-start.1 = ((f32[32,1,196]{2,1,0:T(1,128)}), f32[32,1,196]{2,1,0:T(1,128)S(1)}, u32[]{:S(2)}, u32[]{:S(2)}) async-start(f32[32,1,196]{2,1,0:T(1,128)} %all_to_all.18), calls=%async_computation.1 | async-start | bytes 65536 | tf_op jit(solution)/shard_map/all_to_all | solution.py:176
  15.8 25.8 %gather_fusion = bf16[6144,256]{1,0:T(8,128)(2,1)} fusion(bf16[6144,256]{1,0:T(8,128)(2,1)} %x_ref.1, s32[6144]{0:T(1024)S(1)} %get-tuple-element.14), kind=kCustom, calls=%fused_computation | custom fusion | bytes 6316032 | tf_op jit(solution)/shard_map/gather | solution.py:180
  41.7 6.0 %all-to-all-start = ((bf16[32,192,256]{2,1,0:T(8,128)(2,1)}), bf16[32,192,256]{2,1,0:T(8,128)(2,1)}, u32[]{:S(2)}, u32[]{:S(2)}) async-start(bf16[32,192,256]{2,1,0:T(8,128)(2,1)} %bitcast), calls=%async_computation | async-start | bytes 6291456 | tf_op jit(solution)/shard_map/all_to_all | solution.py:179
  47.6 0.0 copy-start.2
  47.6 0.0 copy-start.7
  47.7 0.0 copy-start.3
  47.7 0.0 copy-start.4
  47.7 0.0 copy-start.5
  47.7 0.1 broadcast_multiply_fusion
  47.9 1.0 mul.32
  48.9 0.8 copy.40.expand_ref
  49.7 0.1 copy.39
  49.8 0.1 copy.38
  50.0 1.0 broadcast_in_dim_tile.4.offset_ref
  50.9 0.1 pad_maximum_fusion.2
  51.0 0.7 copy.43.qkv_ref
  51.7 0.7 pad_maximum_fusion.w_ref
  52.5 0.1 fusion.13
  52.6 0.1 div.28
  52.6 0.1 broadcast_in_dim.42
  52.7 1.0 broadcast_in_dim_reshape.4.scale_ref
  53.7 0.1 convert_element_type.19
  53.8 6.7 %sort.31 = (s32[6144]{0:T(1024)}, s32[6144]{0:T(1024)S(1)}) sort(s32[6144]{0:T(1024)S(1)} %convert_element_type.19, s32[6144]{0:T(1024)S(1)} %iota.22), dimensions={0}, to_apply=%region_2.3 | sort | flops 79872 | bytes 98304 | tf_op jit(solution)/shard_map/sort | solution.py:183
  60.5 17.8 %shard_map.190 = f32[24,512]{1,0:T(8,128)} custom-call(bf16[6144,256]{1,0:T(8,128)(2,1)} %x_ref.1, f32[1,256]{1,0:T(1,128)} %bitcast.35, f32[1,256]{1,0:T(1,128)} %bitcast.37, bf16[512,256]{1,0:T(8,128)(2,1)} %pad_maximum_fusion.w_ref, bf16[512,256]{1,0:T(8,128)(2,1)} %copy.40.expand_ref, f32[512,1]{1,0:T(8,128)} %broadcast_in_dim_tile.4.offset_ref, ...), custom_call_target="tpu_custom_call" | custom-call | flops 6442450944 | bytes 25165824 | tf_op jit(solution)/shard_map/pallas_call | solution.py:197
  78.3 61.7 %psum.7.sums_ref = f32[24,512]{1,0:T(8,128)} all-reduce(f32[24,512]{1,0:T(8,128)} %shard_map.190), channel_id=1, replica_groups=mesh['head'=4,'pts'=8] {'head','pts'}, use_global_device_ids=true, to_apply=%region_1.2 | all-reduce | flops 12288 | bytes 98304 | tf_op jit(solution)/shard_map/psum | solution.py:210
  140.1 44.3 %shard_map.191 = bf16[6144,256]{1,0:T(8,128)(2,1)} custom-call(bf16[6144,256]{1,0:T(8,128)(2,1)} %bitcast.1.x_ref, f32[24,512]{1,0:T(8,128)} %psum.7.sums_ref, f32[48,16]{1,0:T(8,128)} %copy.43.qkv_ref, f32[1,256]{1,0:T(1,128)} %bitcast.36, f32[1,256]{1,0:T(1,128)} %bitcast.38, bf16[256,256]{1,0:T(8,128)(2,1)} %bitcast.26, ...), custom_call_target="tpu_custom_call" | custom-call | flops 12884901888 | bytes 25165824 | tf_op jit(solution)/shard_map/pallas_call | solution.py:221
  184.3 25.8 %gather_fusion.1 = bf16[6144,256]{1,0:T(8,128)(2,1)} fusion(bf16[6144,256]{1,0:T(8,128)(2,1)} %shard_map.191, s32[6144]{0:T(1024)S(1)} %fusion.6), kind=kCustom, calls=%fused_computation.1 | custom fusion | bytes 6316032 | tf_op jit(solution)/shard_map/gather | solution.py:234
  (22 shorter events, 0.1 us)
Async XLA Ops:
  8.5 33.2 %all-to-all-start.1 = ((f32[32,1,196]{2,1,0:T(1,128)}), f32[32,1,196]{2,1,0:T(1,128)S(1)}, u32[]{:S(2)}, u32[]{:S(2)}) async-start(f32[32,1,196]{2,1,0:T(1,128)} %all_to_all.18), calls=%async_computation.1 | async-start | bytes 65536 | tf_op jit(solution)/shard_map/all_to_all | solution.py:176
  41.7 6.0 %copy-start.6 = (bf16[16,32]{1,0:T(8,128)(2,1)S(1)}, bf16[16,32]{1,0:T(8,128)(2,1)}, u32[]{:S(2)}) copy-start(bf16[16,32]{1,0:T(8,128)(2,1)} %param.26) | copy-start | bytes 3076
  41.7 8.1 %copy-start.1 = (bf16[256,256]{1,0:T(8,128)(2,1)S(1)}, bf16[256,256]{1,0:T(8,128)(2,1)}, u32[]{:S(2)}) copy-start(bf16[256,256]{1,0:T(8,128)(2,1)} %param.25) | copy-start | bytes 393220
  41.7 98.4 %all-to-all-start = ((bf16[32,192,256]{2,1,0:T(8,128)(2,1)}), bf16[32,192,256]{2,1,0:T(8,128)(2,1)}, u32[]{:S(2)}, u32[]{:S(2)}) async-start(bf16[32,192,256]{2,1,0:T(8,128)(2,1)} %bitcast), calls=%async_computation | async-start | bytes 6291456 | tf_op jit(solution)/shard_map/all_to_all | solution.py:179
  47.6 2.2 %copy-start.2 = (bf16[256,256]{1,0:T(8,128)(2,1)S(1)}, bf16[256,256]{1,0:T(8,128)(2,1)}, u32[]{:S(2)}) copy-start(bf16[256,256]{1,0:T(8,128)(2,1)} %param.24) | copy-start | bytes 393220
  47.6 2.3 %copy-start.7 = (f32[32]{0:T(128)S(1)}, f32[32]{0:T(128)}, u32[]{:S(2)}) copy-start(f32[32]{0:T(128)} %param.27) | copy-start | bytes 388
  47.7 3.3 %copy-start.3 = (f32[16,16]{1,0:T(8,128)S(1)}, f32[16,16]{1,0:T(8,128)}, u32[]{:S(2)}) copy-start(f32[16,16]{1,0:T(8,128)} %param.31) | copy-start | bytes 3076
  47.7 3.3 %copy-start.4 = (f32[16,16]{1,0:T(8,128)S(1)}, f32[16,16]{1,0:T(8,128)}, u32[]{:S(2)}) copy-start(f32[16,16]{1,0:T(8,128)} %param.30) | copy-start | bytes 3076
  47.7 3.3 %copy-start.5 = (f32[16,16]{1,0:T(8,128)S(1)}, f32[16,16]{1,0:T(8,128)}, u32[]{:S(2)}) copy-start(f32[16,16]{1,0:T(8,128)} %param.29) | copy-start | bytes 3076
  49.8 28.5 %copy-start = (bf16[256,256]{0,1:T(8,128)(2,1)}, bf16[256,256]{0,1:T(8,128)(2,1)S(1)}, u32[]{:S(2)}) copy-start(bf16[256,256]{0,1:T(8,128)(2,1)S(1)} %copy.39) | copy-start | bytes 393220

commit v2 on v1

v2 whole, which is shorter than its diff:
```python
import functools
import math

import jax
import jax.numpy as jnp
from jax import lax
from jax.experimental import pallas as pl
from jax.experimental.pallas import tpu as pltpu
from jax.sharding import PartitionSpec as P

DH = 16
TILE = 512
CHUNKS = 3
F32 = jnp.float32
BF16 = jnp.bfloat16
HIGHEST = lax.Precision.HIGHEST
LOG2E = math.log2(math.e)
NT = (((1,), (1,)), ((), ()))


def norm_rows(rows, gain, bias):
    mean = jnp.mean(rows, axis=-1, keepdims=True)
    centred = rows - mean
    spread = jnp.mean(centred * centred, axis=-1, keepdims=True)
    return (centred * lax.rsqrt(spread + 1e-05) * gain + bias).astype(BF16)


def slice_weights(feeder_t, expand, offset, scale, slices):
    raw = jnp.dot(expand, feeder_t, preferred_element_type=F32)
    logit = (raw + offset) * scale
    lanes = logit.shape[1]
    logit = logit.reshape(-1, slices, lanes)
    powers = jnp.exp2(logit - jnp.max(logit, axis=1, keepdims=True))
    share = powers * (1.0 / jnp.sum(powers, axis=1, keepdims=True))
    return share.reshape(-1, lanes)


def same_head(shape, row_size, column_size):
    row_head = lax.broadcasted_iota(jnp.int32, shape, 0) // row_size
    column_head = lax.broadcasted_iota(jnp.int32, shape, 1) // column_size
    return row_head == column_head


def sums_kernel(
    slices, x_ref, gain_ref, bias_ref, attribute_ref, feeder_ref, project_ref, offset_row_ref,
    sharp_row_ref, out_ref, w_ref, expand_ref, offset_ref, scale_ref, numer, total,
):
    step = pl.program_id(0)
    width = x_ref.shape[1]

    @pl.when(step == 0)
    def _():
        numer[...] = jnp.zeros_like(numer)
        total[...] = jnp.zeros_like(total)
        w_ref[:width] = attribute_ref[...].astype(F32).T.astype(BF16)
        w_ref[width:] = feeder_ref[...].astype(F32).T.astype(BF16)
        columns, heads = offset_ref.shape[0], sharp_row_ref.shape[1]
        stacked = jnp.concatenate([project_ref[...].astype(F32).T] * heads, axis=0)
        lane = lax.broadcasted_iota(jnp.int32, (DH, width), 1) % DH
        pick = (lane == lax.broadcasted_iota(jnp.int32, (DH, width), 0)).astype(BF16)
        filled = jnp.dot(stacked.astype(BF16), pick, preferred_element_type=F32)
        expand_ref[...] = jnp.where(
            same_head(filled.shape, slices, DH), filled, 0.0
        ).astype(BF16)
        own = same_head((columns, heads), slices, 1)
        sharp = jnp.sum(jnp.where(own, sharp_row_ref[...], 0.0), axis=1, keepdims=True)
        scale_ref[...] = LOG2E / sharp
        row = lax.broadcasted_iota(jnp.int32, (columns, slices), 0) % slices
        match = row == lax.broadcasted_iota(jnp.int32, (columns, slices), 1)
        offset_ref[...] = jnp.sum(
            jnp.where(match, offset_row_ref[...], 0.0), axis=1, keepdims=True
        )

    normed = norm_rows(x_ref[...].astype(F32), gain_ref[...], bias_ref[...])
    both = lax.dot_general(w_ref[...], normed, NT, preferred_element_type=F32).astype(BF16)
    share = slice_weights(
        both[width:], expand_ref[...], offset_ref[...], scale_ref[...], slices
    )
    numer[...] += lax.dot_general(
        both[:width], share.astype(BF16), NT, preferred_element_type=F32
    )
    lanes = total.shape[1]
    part = share[:, :lanes]
    for at in range(lanes, share.shape[1], lanes):
        part += share[:, at : at + lanes]
    total[...] += part

    @pl.when(step == pl.num_programs(0) - 1)
    def _():
        kept = jnp.where(same_head(numer.shape, DH, slices), numer[...], 0.0)
        out_ref[:DH] = jnp.sum(kept.reshape(-1, DH, kept.shape[1]), axis=0)
        out_ref[DH:] = lax.dot_general(
            jnp.ones((8, lanes), F32), total[...], NT, precision=HIGHEST,
            preferred_element_type=F32,
        )


def exact_gelu(h):
    half = 0.5 * h
    return half + half * lax.erf(h * (1.0 / math.sqrt(2.0)))


def blend_kernel(slices, sums_ref, question_ref, lookup_ref, content_ref, blend):
    stok = sums_ref[:DH] / (sums_ref[DH : DH + 1] + 1e-05)
    query, key, value = (
        jnp.dot(m[...].T, stok, precision=HIGHEST, preferred_element_type=F32)
        for m in (question_ref, lookup_ref, content_ref)
    )
    scores = jnp.dot(key.T, query, precision=HIGHEST, preferred_element_type=F32)
    scores = scores * (1.0 / math.sqrt(DH))
    mask = same_head(scores.shape, slices, slices)
    scores = jnp.where(mask, scores, -jnp.inf)
    powers = jnp.exp(scores - jnp.max(scores, axis=0, keepdims=True))
    attention = powers / jnp.sum(powers, axis=0, keepdims=True)
    sout = jnp.dot(value, attention, precision=HIGHEST, preferred_element_type=F32)
    spread = jnp.concatenate([sout] * (blend.shape[0] // DH), axis=0)
    blend[...] = jnp.where(same_head(blend.shape, DH, slices), spread, 0.0).astype(BF16)


def rows_kernel(
    slices, x_ref, blend, gain_ref, bias_ref, w_ref, expand_ref, offset_ref,
    scale_ref, emit_ref, emit_bias_ref, gain2_ref, bias2_ref, entry_ref, entry_bias_ref,
    exit_ref, exit_bias_ref, *earlier_and_out,
):
    out_ref = earlier_and_out[-1]
    width = x_ref.shape[1]
    x = x_ref[...].astype(F32)
    normed = norm_rows(x, gain_ref[...], bias_ref[...])
    feeder = lax.dot_general(w_ref[width:], normed, NT, preferred_element_type=F32).astype(BF16)
    share = slice_weights(feeder, expand_ref[...], offset_ref[...], scale_ref[...], slices)
    mixed = jnp.dot(blend[...], share.astype(BF16), preferred_element_type=F32)
    y = (
        x
        + jnp.dot(mixed.T.astype(BF16), emit_ref[...], preferred_element_type=F32)
        + emit_bias_ref[...]
    )
    z = norm_rows(y, gain2_ref[...], bias2_ref[...])
    result = y + exit_bias_ref[...]
    chunk = x_ref.shape[1]
    for at in range(0, entry_ref.shape[1], chunk):
        h = jnp.dot(z, entry_ref[:, at : at + chunk], preferred_element_type=F32)
        g = exact_gelu(h + entry_bias_ref[:, at : at + chunk]).astype(BF16)
        result += jnp.dot(g, exit_ref[at : at + chunk], preferred_element_type=F32)
    out_ref[...] = result.astype(BF16)


def whole(array):
    return pl.BlockSpec(array.shape, lambda i: (0,) * array.ndim)


def body(
    layer_inputs_trainorder,
    inference_placement,
    initial_layernorm_gain,
    initial_layernorm_offset,
    attribute_projection,
    assignment_feeder_projection,
    partition_projection,
    partition_offset,
    softmax_sharpness,
    partition_question_map,
    partition_lookup_map,
    partition_content_map,
    emitted_projection,
    emitted_offset,
    latter_layernorm_gain,
    latter_layernorm_offset,
    perceptron_entry_map,
    perceptron_entry_offset,
    perceptron_exit_map,
    perceptron_exit_offset,
):
    groups = lax.axis_size("head")
    shards = lax.axis_size("pts")
    devices = groups * shards
    both = ("head", "pts")
    local_rows, width = layer_inputs_trainorder.shape
    per_pair = local_rows // devices
    own_heads = softmax_sharpness.shape[0]
    heads = own_heads * groups
    slices = partition_projection.shape[1]
    columns = heads * slices
    chunk_pair = per_pair // CHUNKS
    chunk_rows = chunk_pair * devices
    tile = math.gcd(TILE, chunk_rows)

    sharpness = lax.all_to_all(
        jnp.broadcast_to(softmax_sharpness, (groups, own_heads)), "head", split_axis=0,
        concat_axis=0, tiled=True,
    ).reshape(1, heads)

    dest_block = inference_placement // local_rows
    target = dest_block % groups * shards + dest_block // groups
    send_key = target * local_rows + inference_placement % local_rows
    counting = jnp.arange(local_rows, dtype=jnp.int32)
    send_key, ordering = lax.sort((send_key, counting), num_keys=1)
    ordering = ordering.reshape(devices, CHUNKS, chunk_pair)
    spots = (send_key % local_rows).reshape(devices, per_pair)

    def gathered(order):
        return layer_inputs_trainorder[order.reshape(chunk_rows)]

    def exchange(rows):
        return lax.all_to_all(rows, both, split_axis=0, concat_axis=0, tiled=True)

    arrived = [exchange(gathered(ordering[:, 0]))]
    arrived_spots = exchange(spots).reshape(devices, CHUNKS, chunk_pair)
    arrived_spots = arrived_spots.transpose(1, 0, 2).reshape(local_rows)
    _, placed = lax.sort((arrived_spots, counting), num_keys=1)

    gain = initial_layernorm_gain[None]
    bias = initial_layernorm_offset[None]
    operands = (
        gain, bias, attribute_projection, assignment_feeder_projection, partition_projection,
        partition_offset[None], sharpness,
    )
    made = (
        jax.ShapeDtypeStruct((DH + 8, columns), F32),
        jax.ShapeDtypeStruct((2 * width, width), BF16),
        jax.ShapeDtypeStruct((columns, width), BF16),
        jax.ShapeDtypeStruct((columns, 1), F32),
        jax.ShapeDtypeStruct((columns, 1), F32),
    )
    sums, *constants = pl.pallas_call(
        functools.partial(sums_kernel, slices),
        grid=(local_rows // tile,),
        in_specs=[pl.BlockSpec((tile, width), lambda i: (i, 0))] + [whole(a) for a in operands],
        out_specs=[whole(a) for a in made],
        out_shape=made,
        scratch_shapes=[pltpu.VMEM((width, columns), F32), pltpu.VMEM((columns, 128), F32)],
        compiler_params=pltpu.CompilerParams(dimension_semantics=("arbitrary",)),
        cost_estimate=pl.CostEstimate(
            flops=local_rows * width * columns * 8, bytes_accessed=local_rows * width * 16,
            transcendentals=local_rows * columns,
        ),
    )(layer_inputs_trainorder, *operands)

    waiting, sums = lax.optimization_barrier((gathered(ordering[:, 1]), sums))
    sums = lax.psum(sums, both)
    waiting, later, sums = lax.optimization_barrier((waiting, ordering[:, 2:], sums))
    arrived.append(exchange(waiting))
    for at in range(CHUNKS - 2):
        arrived.append(exchange(gathered(later[:, at])))

    maps = (sums, partition_question_map, partition_lookup_map, partition_content_map)
    blend = pl.pallas_call(
        functools.partial(blend_kernel, slices),
        out_shape=jax.ShapeDtypeStruct((width, columns), BF16),
        cost_estimate=pl.CostEstimate(
            flops=columns * columns * 1000, bytes_accessed=columns * width * 8,
            transcendentals=columns * columns,
        ),
    )(*maps)

    operands = (
        blend, gain, bias, *constants, emitted_projection,
        emitted_offset[None], latter_layernorm_gain[None], latter_layernorm_offset[None],
        perceptron_entry_map, perceptron_entry_offset[None], perceptron_exit_map,
        perceptron_exit_offset[None],
    )
    result = ()
    steps = chunk_rows // tile
    for at in range(CHUNKS):
        result = pl.pallas_call(
            functools.partial(rows_kernel, slices),
            grid=(steps,),
            in_specs=[pl.BlockSpec((tile, width), lambda i: (i, 0))]
            + [whole(a) for a in operands]
            + [pl.BlockSpec(memory_space=pl.ANY) for _ in result],
            out_specs=(pl.BlockSpec((tile, width), lambda i, at=at: (i + at * steps, 0)),),
            out_shape=(jax.ShapeDtypeStruct((local_rows, width), BF16),),
            input_output_aliases={1 + len(operands): 0} if result else {},
            compiler_params=pltpu.CompilerParams(dimension_semantics=("arbitrary",)),
            cost_estimate=pl.CostEstimate(
                flops=chunk_rows * width * columns * 16, bytes_accessed=chunk_rows * width * 16,
                transcendentals=chunk_rows * columns * 4,
            ),
        )(arrived[at], *operands, *result)
    return result[0][placed][None]


def solution(mesh):
    placed = (
        P(("head", "pts"), None),
        P(("head", "pts")),
        P(),
        P(),
        P(),
        P(),
        P(),
        P(),
        P("head"),
        P(),
        P(),
        P(),
        P(),
        P(),
        P(),
        P(),
        P(),
        P(),
        P(),
        P(),
    )
    return jax.shard_map(
        body, mesh=mesh, in_specs=placed, out_specs=P("pts", "head", None), check_vma=False
    )
```

time: 211 us -> 218 us (1.033)
  blocking collectives: 61.7 us -> 41.3 us
  waiting for transfers between devices: 0.01 us -> 15.8 us
  starting transfers between devices: 13.3 us -> 26.8 us
  Pallas kernels: 62.1 us -> 57.8 us
    psum x1, blocking collectives: 61.7 us -> 41.3 us  [body(): sums = lax.psum(sums, both)]
    all_to_all x2 -> x5, waiting for transfers between devices: 0.01 us -> 15.8 us  [the longest x4 15.8 us: exchange(): return lax.all_to_all(rows, both, split_axis=0, concat_axis=0, tiled=True)]
    all_to_all x2 -> x5, starting transfers between devices: 13.3 us -> 26.8 us  [the longest x4 20.4 us: exchange(): return lax.all_to_all(rows, both, split_axis=0, concat_axis=0, tiled=True)]
    pallas_call x1 -> x4, Pallas kernels: 44.3 us -> 39.2 us  [the longest x3 35.7 us: body(): pl.pallas_call(functools.partial(rows_kernel, slices), grid=(steps,), in_...]
    gather x2 -> x4, local copies, waits for them, and re-layouts: 51.7 us -> 54.8 us  [the longest x3 29 us: gathered(): return layer_inputs_trainorder[order.reshape(chunk_rows)]]
  transfers between devices with their start and end apart: 2 -> 5, of which waited for: 0 -> 1; matrix products, arithmetic and copies ran while one was open for 18% -> 21% of each run, Pallas kernels for 8% -> 21%
where the time goes in v2:
time: 218 us; the launch traced here: 217 us
  local copies, waits for them, and re-layouts  60 us (28%)
  Pallas kernels  57.8 us (27%)
  blocking collectives  41.3 us (19%)
  starting transfers between devices  26.8 us (12%)
  waiting for transfers between devices  15.8 us (7%)
  other arithmetic  15.3 us (7%)
    psum x1, blocking collectives, body(): sums = lax.psum(sums, both)  41.3 us
    pallas_call x3, Pallas kernels, body(): pl.pallas_call(functools.partial(rows_kernel, slices), grid=(steps,), in_...  35.7 us
    gather x3, local copies, waits for them, and re-layouts, gathered(): return layer_inputs_trainorder[order.reshape(chunk_rows)]  29 us
    gather x1, local copies, waits for them, and re-layouts, body(): return result[0][placed][None]  25.8 us
    all_to_all x4, starting transfers between devices, exchange(): return lax.all_to_all(rows, both, split_axis=0, concat_axis=0, tiled=True)  20.4 us
    pallas_call x1, Pallas kernels, body(): pl.pallas_call(functools.partial(sums_kernel, slices), grid=(local_rows /...  18.6 us
    all_to_all x4, waiting for transfers between devices, exchange(): return lax.all_to_all(rows, both, split_axis=0, concat_axis=0, tiled=True)  15.8 us
    sort x1, other arithmetic, body(): _, placed = lax.sort((arrived_spots, counting), num_keys=1)  6.72 us
  transfers between devices with their start and end apart: 5, of which 1 were waited for; matrix products, arithmetic and copies ran while one was open for 21% of the time, Pallas kernels for 21%

profile of v2, /device:TPU:0, one launch (start us, length us, event | category | flops | bytes accessed | tf_op | source)
XLA Modules:
  0.0 217.2 jit_solution(15053161387506217765)
XLA Ops:
  0.0 1.2 broadcast_in_dim.39
  1.2 6.3 %all-to-all-start = ((f32[4,1,4]{2,1,0:T(1,128)}), f32[4,1,4]{2,1,0:T(1,128)S(1)}, u32[]{:S(2)}, u32[]{:S(2)}) async-start(f32[4,1,4]{2,1,0:T(1,128)} %broadcast_in_dim.39), calls=%async_computation | async-start | bytes 4096 | tf_op jit(solution)/shard_map/all_to_all | solution.py:187
  7.6 0.8 fusion.3
  8.4 6.2 %sort.30 = (s32[6144]{0:T(1024)S(1)}, s32[6144]{0:T(1024)S(1)}) sort(s32[6144]{0:T(1024)S(1)} %fusion.3, s32[6144]{0:T(1024)S(1)} %iota.5), dimensions={0}, to_apply=%region_0.1 | sort | flops 79872 | bytes 98304 | tf_op jit(solution)/shard_map/sort | solution.py:196
  14.6 0.1 reshape.112
  14.7 0.1 slice_reduce_fusion
  14.8 0.1 reshape_squeeze.11
  14.9 0.7 all_to_all.41
  15.6 6.1 %all-to-all-start.4 = ((s32[32,1,192]{2,1,0:T(1,128)}), s32[32,1,192]{2,1,0:T(1,128)S(1)}, u32[]{:S(2)}, u32[]{:S(2)}) async-start(s32[32,1,192]{2,1,0:T(1,128)} %all_to_all.41), calls=%async_computation.4 | async-start | bytes 65536 | tf_op jit(solution)/shard_map/all_to_all | solution.py:204
  21.7 10.9 %gather_fusion.2 = bf16[2048,256]{1,0:T(8,128)(2,1)} fusion(bf16[6144,256]{1,0:T(8,128)(2,1)} %x_ref.1, s32[2048]{0:T(1024)S(1)} %broadcast_clamp_fusion), kind=kCustom, calls=%fused_computation.2 | custom fusion | bytes 2105344 | tf_op jit(solution)/shard_map/gather | solution.py:201
  32.7 6.0 %all-to-all-start.3 = ((bf16[32,64,256]{2,1,0:T(8,128)(2,1)}), bf16[32,64,256]{2,1,0:T(8,128)(2,1)}, u32[]{:S(2)}, u32[]{:S(2)}) async-start(bf16[32,64,256]{2,1,0:T(8,128)(2,1)} %bitcast.21), calls=%async_computation.3 | async-start | bytes 2097152 | tf_op jit(solution)/shard_map/all_to_all | solution.py:204
  38.6 0.1 reshape_squeeze.9
  38.8 9.0 %gather_fusion = bf16[2048,256]{1,0:T(8,128)(2,1)} fusion(bf16[6144,256]{1,0:T(8,128)(2,1)S(1)} %copy-done, s32[2048]{0:T(1024)S(1)} %broadcast_clamp_fusion.1), kind=kCustom, calls=%fused_computation | custom fusion | bytes 2105344 | tf_op jit(solution)/shard_map/gather | solution.py:201
  47.8 0.6 broadcast.101
  48.3 0.7 reduce.15
  49.1 0.6 reshape.113.sharp_row_ref
  49.6 18.6 %shard_map.190 = (f32[24,512]{1,0:T(8,128)}, bf16[512,256]{1,0:T(8,128)(2,1)}, bf16[512,256]{1,0:T(8,128)(2,1)}, f32[512,1]{1,0:T(8,128)}, f32[512,1]{1,0:T(8,128)}) custom-call(bf16[6144,256]{1,0:T(8,128)(2,1)} %x_ref.1, f32[1,256]{1,0:T(1,128)} %bitcast.30, f32[1,256]{1,0:T(1,128)} %bitcast.34, bf16[256,256]{1,0:T(8,128)(2,1)} %attribute_ref.1, ...), custom_call_target="tpu_custom_call" | custom-call | flops 6442450944 | bytes 25165824 | tf_op jit(solution)/shard_map/pallas_call | solution.py:224
  68.3 41.3 %psum.7.sums_ref = f32[24,512]{1,0:T(8,128)} all-reduce(f32[24,512]{1,0:T(8,128)} %get-tuple-element.21), channel_id=1, replica_groups=mesh['head'=4,'pts'=8] {'head','pts'}, use_global_device_ids=true, to_apply=%region_1.2 | all-reduce | flops 12288 | bytes 98304 | tf_op jit(solution)/shard_map/psum | solution.py:239
  109.6 4.6 %all-to-all-start.2 = ((bf16[32,64,256]{2,1,0:T(8,128)(2,1)}), bf16[32,64,256]{2,1,0:T(8,128)(2,1)}, u32[]{:S(2)}, u32[]{:S(2)}) async-start(bf16[32,64,256]{2,1,0:T(8,128)(2,1)} %bitcast.19), calls=%async_computation.2 | async-start | bytes 2097152 | tf_op jit(solution)/shard_map/all_to_all | solution.py:204
  114.2 0.5 broadcast.102
  114.7 0.7 reduce.16
  115.5 9.1 %gather_fusion.1 = bf16[2048,256]{1,0:T(8,128)(2,1)} fusion(bf16[6144,256]{1,0:T(8,128)(2,1)S(1)} %copy-done.1, s32[2048]{0:T(1024)S(1)} %broadcast_clamp_fusion.2), kind=kCustom, calls=%fused_computation.1 | custom fusion | bytes 2105344 | tf_op jit(solution)/shard_map/gather | solution.py:201
  124.5 15.8 %all-to-all-done.2 = bf16[32,64,256]{2,1,0:T(8,128)(2,1)} async-done(((bf16[32,64,256]{2,1,0:T(8,128)(2,1)}), bf16[32,64,256]{2,1,0:T(8,128)(2,1)}, u32[]{:S(2)}, u32[]{:S(2)}) %all-to-all-start.2) | async-done | bytes 1048608 | tf_op jit(solution)/shard_map/all_to_all | solution.py:204
  140.3 3.8 %all-to-all-start.1 = ((bf16[32,64,256]{2,1,0:T(8,128)(2,1)}), bf16[32,64,256]{2,1,0:T(8,128)(2,1)S(1)}, u32[]{:S(2)}, u32[]{:S(2)}) async-start(bf16[32,64,256]{2,1,0:T(8,128)(2,1)} %bitcast.20), calls=%async_computation.1 | async-start | bytes 2097152 | tf_op jit(solution)/shard_map/all_to_all | solution.py:204
  144.1 3.5 %shard_map.191.blend = bf16[256,512]{1,0:T(8,128)(2,1)} custom-call(f32[24,512]{1,0:T(8,128)} %psum.7.sums_ref, f32[16,16]{1,0:T(8,128)} %question_ref.1, f32[16,16]{1,0:T(8,128)} %lookup_ref.1, f32[16,16]{1,0:T(8,128)} %content_ref.1), custom_call_target="tpu_custom_call" | custom-call | flops 262144000 | bytes 1048576 | tf_op jit(solution)/shard_map/pallas_call | solution.py:246
  147.7 0.1 reshape.114
  147.9 6.7 %sort.31 = (s32[6144]{0:T(1024)}, s32[6144]{0:T(1024)S(1)}) sort(s32[6144]{0:T(1024)S(1)} %reshape.115, s32[6144]{0:T(1024)S(1)} %iota.6), dimensions={0}, to_apply=%region_2.3 | sort | flops 79872 | bytes 98304 | tf_op jit(solution)/shard_map/sort | solution.py:209
  154.7 11.9 %shard_map.192.earlier_and_out_0_ = bf16[6144,256]{1,0:T(8,128)(2,1)} custom-call(bf16[2048,256]{1,0:T(8,128)(2,1)} %bitcast.16.x_ref, bf16[256,512]{1,0:T(8,128)(2,1)} %shard_map.191.blend, f32[1,256]{1,0:T(1,128)} %bitcast.31, f32[1,256]{1,0:T(1,128)} %bitcast.35, bf16[512,256]{1,0:T(8,128)(2,1)} %get-tuple-element.24.w_ref, ...), custom_call_target="tpu_custom_call" | custom-call | flops 4294967296 | bytes 8388608 | tf_op jit(solution)/shard_map/pallas_call | solution.py:264
  166.6 11.9 %shard_map.193.earlier_and_out_0_ = bf16[6144,256]{1,0:T(8,128)(2,1)} custom-call(bf16[2048,256]{1,0:T(8,128)(2,1)} %bitcast.13.x_ref, bf16[256,512]{1,0:T(8,128)(2,1)} %shard_map.191.blend, f32[1,256]{1,0:T(1,128)} %bitcast.32, f32[1,256]{1,0:T(1,128)} %bitcast.36, bf16[512,256]{1,0:T(8,128)(2,1)} %get-tuple-element.24.w_ref, ...), custom_call_target="tpu_custom_call", output_to_operand_aliasing={{}: (16, {})} | custom-call | flops 4294967296 | bytes 8388608 | tf_op jit(solution)/shard_map/pallas_call | solution.py:264
  178.5 1.0 copy-done.2
  179.5 11.9 %shard_map.194 = bf16[6144,256]{1,0:T(8,128)(2,1)} custom-call(bf16[2048,256]{1,0:T(8,128)(2,1)} %bitcast.22, bf16[256,512]{1,0:T(8,128)(2,1)} %shard_map.191.blend, f32[1,256]{1,0:T(1,128)} %bitcast.33, f32[1,256]{1,0:T(1,128)} %bitcast.37, bf16[512,256]{1,0:T(8,128)(2,1)} %get-tuple-element.24.w_ref, ...), custom_call_target="tpu_custom_call", output_to_operand_aliasing={{}: (16, {})} | custom-call | flops 4294967296 | bytes 8388608 | tf_op jit(solution)/shard_map/pallas_call | solution.py:264
  191.3 25.8 %gather_fusion.3 = bf16[6144,256]{1,0:T(8,128)(2,1)} fusion(bf16[6144,256]{1,0:T(8,128)(2,1)} %shard_map.194, s32[6144]{0:T(1024)S(1)} %fusion.4), kind=kCustom, calls=%fused_computation.3 | custom fusion | bytes 6316032 | tf_op jit(solution)/shard_map/gather | solution.py:279
  (23 shorter events, 0.3 us)
Async XLA Ops:
  1.2 14.4 %all-to-all-start = ((f32[4,1,4]{2,1,0:T(1,128)}), f32[4,1,4]{2,1,0:T(1,128)S(1)}, u32[]{:S(2)}, u32[]{:S(2)}) async-start(f32[4,1,4]{2,1,0:T(1,128)} %broadcast_in_dim.39), calls=%async_computation | async-start | bytes 4096 | tf_op jit(solution)/shard_map/all_to_all | solution.py:187
  15.6 17.1 %all-to-all-start.4 = ((s32[32,1,192]{2,1,0:T(1,128)}), s32[32,1,192]{2,1,0:T(1,128)S(1)}, u32[]{:S(2)}, u32[]{:S(2)}) async-start(s32[32,1,192]{2,1,0:T(1,128)} %all_to_all.41), calls=%async_computation.4 | async-start | bytes 65536 | tf_op jit(solution)/shard_map/all_to_all | solution.py:204
  21.7 17.0 %copy-start = (bf16[6144,256]{1,0:T(8,128)(2,1)S(1)}, bf16[6144,256]{1,0:T(8,128)(2,1)}, u32[]{:S(2)}) copy-start(bf16[6144,256]{1,0:T(8,128)(2,1)} %x_ref.1) | copy-start | bytes 9437188
  32.7 76.9 %all-to-all-start.3 = ((bf16[32,64,256]{2,1,0:T(8,128)(2,1)}), bf16[32,64,256]{2,1,0:T(8,128)(2,1)}, u32[]{:S(2)}, u32[]{:S(2)}) async-start(bf16[32,64,256]{2,1,0:T(8,128)(2,1)} %bitcast.21), calls=%async_computation.3 | async-start | bytes 2097152 | tf_op jit(solution)/shard_map/all_to_all | solution.py:204
  49.6 65.8 %copy-start.1 = (bf16[6144,256]{1,0:T(8,128)(2,1)S(1)}, bf16[6144,256]{1,0:T(8,128)(2,1)}, u32[]{:S(2)}) copy-start(bf16[6144,256]{1,0:T(8,128)(2,1)} %x_ref.1) | copy-start | bytes 9437188
  109.6 30.8 %all-to-all-start.2 = ((bf16[32,64,256]{2,1,0:T(8,128)(2,1)}), bf16[32,64,256]{2,1,0:T(8,128)(2,1)}, u32[]{:S(2)}, u32[]{:S(2)}) async-start(bf16[32,64,256]{2,1,0:T(8,128)(2,1)} %bitcast.19), calls=%async_computation.2 | async-start | bytes 2097152 | tf_op jit(solution)/shard_map/all_to_all | solution.py:204
  140.3 38.1 %all-to-all-start.1 = ((bf16[32,64,256]{2,1,0:T(8,128)(2,1)}), bf16[32,64,256]{2,1,0:T(8,128)(2,1)S(1)}, u32[]{:S(2)}, u32[]{:S(2)}) async-start(bf16[32,64,256]{2,1,0:T(8,128)(2,1)} %bitcast.20), calls=%async_computation.1 | async-start | bytes 2097152 | tf_op jit(solution)/shard_map/all_to_all | solution.py:204
  178.5 1.0 copy-start.2

commit v3 on v2

--- a/solution.py
+++ b/solution.py
@@ -184,18 +184,16 @@
     chunk_rows = chunk_pair * devices
     tile = math.gcd(TILE, chunk_rows)
 
-    sharpness = lax.all_to_all(
-        jnp.broadcast_to(softmax_sharpness, (groups, own_heads)), "head", split_axis=0,
-        concat_axis=0, tiled=True,
-    ).reshape(1, heads)
-
     dest_block = inference_placement // local_rows
     target = dest_block % groups * shards + dest_block // groups
     send_key = target * local_rows + inference_placement % local_rows
     counting = jnp.arange(local_rows, dtype=jnp.int32)
     send_key, ordering = lax.sort((send_key, counting), num_keys=1)
     ordering = ordering.reshape(devices, CHUNKS, chunk_pair)
-    spots = (send_key % local_rows).reshape(devices, per_pair)
+    spots = (send_key % local_rows).astype(F32).reshape(devices, per_pair)
+    small = jnp.concatenate(
+        [spots, jnp.broadcast_to(softmax_sharpness, (devices, own_heads))], axis=1
+    )
 
     def gathered(order):
         return layer_inputs_trainorder[order.reshape(chunk_rows)]
@@ -204,7 +202,9 @@
         return lax.all_to_all(rows, both, split_axis=0, concat_axis=0, tiled=True)
 
     arrived = [exchange(gathered(ordering[:, 0]))]
-    arrived_spots = exchange(spots).reshape(devices, CHUNKS, chunk_pair)
+    small = exchange(small)
+    sharpness = small.reshape(groups, shards, -1)[:, 0, per_pair:].reshape(1, heads)
+    arrived_spots = small[:, :per_pair].astype(jnp.int32).reshape(devices, CHUNKS, chunk_pair)
     arrived_spots = arrived_spots.transpose(1, 0, 2).reshape(local_rows)
     _, placed = lax.sort((arrived_spots, counting), num_keys=1)
 
@@ -235,12 +235,14 @@
         ),
     )(layer_inputs_trainorder, *operands)
 
-    waiting, sums = lax.optimization_barrier((gathered(ordering[:, 1]), sums))
-    sums = lax.psum(sums, both)
+    waiting, sums, arrived[0] = lax.optimization_barrier(
+        (gathered(ordering[:, 1]), sums, arrived[0])
+    )
+    part = jnp.sum(exchange(sums.reshape(devices, -1)), axis=0)
+    sums = exchange(jnp.broadcast_to(part, (devices,) + part.shape)).reshape(sums.shape)
     waiting, later, sums = lax.optimization_barrier((waiting, ordering[:, 2:], sums))
     arrived.append(exchange(waiting))
-    for at in range(CHUNKS - 2):
-        arrived.append(exchange(gathered(later[:, at])))
+    later = [gathered(later[:, at]) for at in range(CHUNKS - 2)]
 
     maps = (sums, partition_question_map, partition_lookup_map, partition_content_map)
     blend = pl.pallas_call(
@@ -276,6 +278,9 @@
                 transcendentals=chunk_rows * columns * 4,
             ),
         )(arrived[at], *operands, *result)
+        if at + 2 < CHUNKS:
+            leaving, result = lax.optimization_barrier((later[at], result))
+            arrived.append(exchange(leaving))
     return result[0][placed][None]
 
 

time: 218 us -> 186 us (0.85)
  blocking collectives: 41.3 us -> 21.9 us
  waiting for transfers between devices: 15.8 us -> 7.55 us
  starting transfers between devices: 26.8 us -> 22.2 us
    psum x1 -> x0, blocking collectives: 41.3 us -> none  [body(): sums = lax.psum(sums, both)]
    all_to_all x0 -> x2, blocking collectives: none -> 21.9 us  [exchange(): return lax.all_to_all(rows, both, split_axis=0, concat_axis=0, tiled=True)]
    all_to_all x4, waiting for transfers between devices: 15.8 us -> 7.55 us  [exchange(): return lax.all_to_all(rows, both, split_axis=0, concat_axis=0, tiled=True)]
    all_to_all x1 -> x0, starting transfers between devices: 6.35 us -> none  [body(): lax.all_to_all(jnp.broadcast_to(softmax_sharpness, (groups, own_heads)),...]
  transfers between devices with their start and end apart: 5 -> 4, of which waited for: 1 -> 2; matrix products, arithmetic and copies ran while one was open for 21% -> 21% of each run, Pallas kernels for 21% -> 25%
where the time goes in v3:
time: 186 us; the launch traced here: 185 us
  local copies, waits for them, and re-layouts  60.6 us (33%)
  Pallas kernels  57.8 us (31%)
  starting transfers between devices  22.2 us (12%)
  blocking collectives  21.9 us (12%)
  other arithmetic  14.7 us (8%)
  waiting for transfers between devices  7.55 us (4%)
    pallas_call x3, Pallas kernels, body(): pl.pallas_call(functools.partial(rows_kernel, slices), grid=(steps,), in_...  35.7 us
    gather x3, local copies, waits for them, and re-layouts, gathered(): return layer_inputs_trainorder[order.reshape(chunk_rows)]  29 us
    gather x1, local copies, waits for them, and re-layouts, body(): return result[0][placed][None]  25.8 us
    all_to_all x4, starting transfers between devices, exchange(): return lax.all_to_all(rows, both, split_axis=0, concat_axis=0, tiled=True)  22.2 us
    all_to_all x2, blocking collectives, exchange(): return lax.all_to_all(rows, both, split_axis=0, concat_axis=0, tiled=True)  21.9 us
    pallas_call x1, Pallas kernels, body(): pl.pallas_call(functools.partial(sums_kernel, slices), grid=(local_rows /...  18.6 us
    all_to_all x4, waiting for transfers between devices, exchange(): return lax.all_to_all(rows, both, split_axis=0, concat_axis=0, tiled=True)  7.55 us
    sort x1, other arithmetic, body(): _, placed = lax.sort((arrived_spots, counting), num_keys=1)  6.72 us
  transfers between devices with their start and end apart: 4, of which 2 were waited for; matrix products, arithmetic and copies ran while one was open for 21% of the time, Pallas kernels for 25%

profile of v3, /device:TPU:0, one launch (start us, length us, event | category | flops | bytes accessed | tf_op | source)
XLA Modules:
  0.0 184.9 jit_solution(6450228689835169926)
XLA Ops:
  0.0 0.8 fusion.3
  0.8 6.2 %sort.30 = (s32[6144]{0:T(1024)S(1)}, s32[6144]{0:T(1024)S(1)}) sort(s32[6144]{0:T(1024)S(1)} %fusion.3, s32[6144]{0:T(1024)S(1)} %iota.5), dimensions={0}, to_apply=%region_0.1 | sort | flops 79872 | bytes 98304 | tf_op jit(solution)/shard_map/sort | solution.py:191
  7.1 0.7 pad.1.clone
  7.9 0.6 all_to_all.40
  8.5 7.3 %all-to-all-start = ((f32[32,1,196]{2,1,0:T(1,128)}), f32[32,1,196]{2,1,0:T(1,128)S(1)}, u32[]{:S(2)}, u32[]{:S(2)}) async-start(f32[32,1,196]{2,1,0:T(1,128)} %all_to_all.40), calls=%async_computation | async-start | bytes 65536 | tf_op jit(solution)/shard_map/all_to_all | solution.py:202
  15.8 0.1 reshape.120
  15.9 0.1 slice_reduce_fusion
  16.1 10.9 %gather_fusion.1 = bf16[2048,256]{1,0:T(8,128)(2,1)} fusion(bf16[6144,256]{1,0:T(8,128)(2,1)} %x_ref.1, s32[2048]{0:T(1024)S(1)} %broadcast_clamp_fusion), kind=kCustom, calls=%fused_computation.1 | custom fusion | bytes 2105344 | tf_op jit(solution)/shard_map/gather | solution.py:199
  27.1 6.0 %all-to-all-start.1 = ((bf16[32,64,256]{2,1,0:T(8,128)(2,1)}), bf16[32,64,256]{2,1,0:T(8,128)(2,1)}, u32[]{:S(2)}, u32[]{:S(2)}) async-start(bf16[32,64,256]{2,1,0:T(8,128)(2,1)} %bitcast.25), calls=%async_computation.1 | async-start | bytes 2097152 | tf_op jit(solution)/shard_map/all_to_all | solution.py:202
  33.2 9.0 %gather_fusion = bf16[2048,256]{1,0:T(8,128)(2,1)} fusion(bf16[6144,256]{1,0:T(8,128)(2,1)S(1)} %copy-done, s32[2048]{0:T(1024)S(1)} %broadcast_clamp_fusion.1), kind=kCustom, calls=%fused_computation | custom fusion | bytes 2105344 | tf_op jit(solution)/shard_map/gather | solution.py:199
  42.2 0.1 slice_reduce_fusion.2
  42.3 0.6 reshape_squeeze.13.sharp_row_ref
  42.9 18.6 %shard_map.190 = (f32[24,512]{1,0:T(8,128)}, bf16[512,256]{1,0:T(8,128)(2,1)}, bf16[512,256]{1,0:T(8,128)(2,1)}, f32[512,1]{1,0:T(8,128)}, f32[512,1]{1,0:T(8,128)}) custom-call(bf16[6144,256]{1,0:T(8,128)(2,1)} %x_ref.1, f32[1,256]{1,0:T(1,128)} %bitcast.36, f32[1,256]{1,0:T(1,128)} %bitcast.40, bf16[256,256]{1,0:T(8,128)(2,1)} %attribute_ref.1, ...), custom_call_target="tpu_custom_call" | custom-call | flops 6442450944 | bytes 25165824 | tf_op jit(solution)/shard_map/pallas_call | solution.py:224
  61.5 0.9 all_to_all.55
  62.3 12.9 %all_to_all.62 = f32[32,1,384]{2,1,0:T(1,128)S(1)} all-to-all(f32[32,1,384]{2,1,0:T(1,128)S(1)} %all_to_all.55), channel_id=1, replica_groups=mesh['head'=4,'pts'=8] {'head','pts'}, dimensions={0} | all-to-all | bytes 98304 | tf_op jit(solution)/shard_map/all_to_all | solution.py:202
  75.3 9.0 %all_to_all.63 = f32[32,1,384]{2,1,0:T(1,128)S(1)} all-to-all(f32[32,1,384]{2,1,0:T(1,128)S(1)} %broadcast_in_dim.43), channel_id=1, replica_groups=mesh['head'=4,'pts'=8] {'head','pts'}, dimensions={0} | all-to-all | bytes 98304 | tf_op jit(solution)/shard_map/all_to_all | solution.py:202
  84.4 0.1 reduce.4
  84.5 0.6 reshape.123.sums_ref
  85.1 3.4 %all-to-all-start.5 = ((bf16[32,64,256]{2,1,0:T(8,128)(2,1)}), bf16[32,64,256]{2,1,0:T(8,128)(2,1)}, u32[]{:S(2)}, u32[]{:S(2)}) async-start(bf16[32,64,256]{2,1,0:T(8,128)(2,1)} %bitcast.24), calls=%async_computation.5 | async-start | bytes 2097152 | tf_op jit(solution)/shard_map/all_to_all | solution.py:202
  88.5 0.5 broadcast.103
  89.0 0.7 reduce.17
  89.8 9.1 %gather_fusion.2 = bf16[2048,256]{1,0:T(8,128)(2,1)} fusion(bf16[6144,256]{1,0:T(8,128)(2,1)S(1)} %copy-done.1, s32[2048]{0:T(1024)S(1)} %broadcast_clamp_fusion.2), kind=kCustom, calls=%fused_computation.2 | custom fusion | bytes 2105344 | tf_op jit(solution)/shard_map/gather | solution.py:199
  98.9 3.5 %shard_map.191.blend = bf16[256,512]{1,0:T(8,128)(2,1)} custom-call(f32[24,512]{1,0:T(8,128)} %reshape.123.sums_ref, f32[16,16]{1,0:T(8,128)} %question_ref.1, f32[16,16]{1,0:T(8,128)} %lookup_ref.1, f32[16,16]{1,0:T(8,128)} %content_ref.1), custom_call_target="tpu_custom_call" | custom-call | flops 262144000 | bytes 1048576 | tf_op jit(solution)/shard_map/pallas_call | solution.py:248
  102.4 11.9 %shard_map.192.earlier_and_out_0_ = bf16[6144,256]{1,0:T(8,128)(2,1)} custom-call(bf16[2048,256]{1,0:T(8,128)(2,1)} %bitcast.6.x_ref, bf16[256,512]{1,0:T(8,128)(2,1)} %shard_map.191.blend, f32[1,256]{1,0:T(1,128)} %bitcast.37, f32[1,256]{1,0:T(1,128)} %bitcast.41, bf16[512,256]{1,0:T(8,128)(2,1)} %get-tuple-element.29.w_ref, ...), custom_call_target="tpu_custom_call" | custom-call | flops 4294967296 | bytes 8388608 | tf_op jit(solution)/shard_map/pallas_call | solution.py:266
  114.3 0.4 all-to-all-done.5
  114.7 5.6 %all-to-all-start.4 = ((bf16[32,64,256]{2,1,0:T(8,128)(2,1)}), bf16[32,64,256]{2,1,0:T(8,128)(2,1)S(1)}, u32[]{:S(2)}, u32[]{:S(2)}) async-start(bf16[32,64,256]{2,1,0:T(8,128)(2,1)} %bitcast.13), calls=%async_computation.4 | async-start | bytes 2097152 | tf_op jit(solution)/shard_map/all_to_all | solution.py:202
  120.4 6.7 %sort.31 = (s32[6144]{0:T(1024)}, s32[6144]{0:T(1024)S(1)}) sort(s32[6144]{0:T(1024)S(1)} %reshape.125, s32[6144]{0:T(1024)S(1)} %iota.6), dimensions={0}, to_apply=%region_2.3 | sort | flops 79872 | bytes 98304 | tf_op jit(solution)/shard_map/sort | solution.py:209
  127.2 11.9 %shard_map.193.earlier_and_out_0_ = bf16[6144,256]{1,0:T(8,128)(2,1)} custom-call(bf16[2048,256]{1,0:T(8,128)(2,1)} %bitcast.16.x_ref, bf16[256,512]{1,0:T(8,128)(2,1)} %shard_map.191.blend, f32[1,256]{1,0:T(1,128)} %bitcast.38, f32[1,256]{1,0:T(1,128)} %bitcast.42, bf16[512,256]{1,0:T(8,128)(2,1)} %get-tuple-element.29.w_ref, ...), custom_call_target="tpu_custom_call", output_to_operand_aliasing={{}: (16, {})} | custom-call | flops 4294967296 | bytes 8388608 | tf_op jit(solution)/shard_map/pallas_call | solution.py:266
  139.1 7.2 %all-to-all-done.4 = bf16[32,64,256]{2,1,0:T(8,128)(2,1)S(1)} async-done(((bf16[32,64,256]{2,1,0:T(8,128)(2,1)}), bf16[32,64,256]{2,1,0:T(8,128)(2,1)S(1)}, u32[]{:S(2)}, u32[]{:S(2)}) %all-to-all-start.4) | async-done | bytes 1048608 | tf_op jit(solution)/shard_map/all_to_all | solution.py:202
  146.3 1.0 copy-done.2
  147.2 11.9 %shard_map.194 = bf16[6144,256]{1,0:T(8,128)(2,1)} custom-call(bf16[2048,256]{1,0:T(8,128)(2,1)} %bitcast.26, bf16[256,512]{1,0:T(8,128)(2,1)} %shard_map.191.blend, f32[1,256]{1,0:T(1,128)} %bitcast.39, f32[1,256]{1,0:T(1,128)} %bitcast.43, bf16[512,256]{1,0:T(8,128)(2,1)} %get-tuple-element.29.w_ref, ...), custom_call_target="tpu_custom_call", output_to_operand_aliasing={{}: (16, {})} | custom-call | flops 4294967296 | bytes 8388608 | tf_op jit(solution)/shard_map/pallas_call | solution.py:266
  159.1 25.8 %gather_fusion.3 = bf16[6144,256]{1,0:T(8,128)(2,1)} fusion(bf16[6144,256]{1,0:T(8,128)(2,1)} %shard_map.194, s32[6144]{0:T(1024)S(1)} %fusion.5), kind=kCustom, calls=%fused_computation.3 | custom fusion | bytes 6316032 | tf_op jit(solution)/shard_map/gather | solution.py:284
  (29 shorter events, 0.7 us)
Async XLA Ops:
  8.5 18.6 %all-to-all-start = ((f32[32,1,196]{2,1,0:T(1,128)}), f32[32,1,196]{2,1,0:T(1,128)S(1)}, u32[]{:S(2)}, u32[]{:S(2)}) async-start(f32[32,1,196]{2,1,0:T(1,128)} %all_to_all.40), calls=%async_computation | async-start | bytes 65536 | tf_op jit(solution)/shard_map/all_to_all | solution.py:202
  16.1 17.0 %copy-start = (bf16[6144,256]{1,0:T(8,128)(2,1)S(1)}, bf16[6144,256]{1,0:T(8,128)(2,1)}, u32[]{:S(2)}) copy-start(bf16[6144,256]{1,0:T(8,128)(2,1)} %x_ref.1) | copy-start | bytes 9437188
  27.1 34.4 %all-to-all-start.1 = ((bf16[32,64,256]{2,1,0:T(8,128)(2,1)}), bf16[32,64,256]{2,1,0:T(8,128)(2,1)}, u32[]{:S(2)}, u32[]{:S(2)}) async-start(bf16[32,64,256]{2,1,0:T(8,128)(2,1)} %bitcast.25), calls=%async_computation.1 | async-start | bytes 2097152 | tf_op jit(solution)/shard_map/all_to_all | solution.py:202
  42.9 46.9 %copy-start.1 = (bf16[6144,256]{1,0:T(8,128)(2,1)S(1)}, bf16[6144,256]{1,0:T(8,128)(2,1)}, u32[]{:S(2)}) copy-start(bf16[6144,256]{1,0:T(8,128)(2,1)} %x_ref.1) | copy-start | bytes 9437188
  85.1 29.5 %all-to-all-start.5 = ((bf16[32,64,256]{2,1,0:T(8,128)(2,1)}), bf16[32,64,256]{2,1,0:T(8,128)(2,1)}, u32[]{:S(2)}, u32[]{:S(2)}) async-start(bf16[32,64,256]{2,1,0:T(8,128)(2,1)} %bitcast.24), calls=%async_computation.5 | async-start | bytes 2097152 | tf_op jit(solution)/shard_map/all_to_all | solution.py:202
  114.7 31.6 %all-to-all-start.4 = ((bf16[32,64,256]{2,1,0:T(8,128)(2,1)}), bf16[32,64,256]{2,1,0:T(8,128)(2,1)S(1)}, u32[]{:S(2)}, u32[]{:S(2)}) async-start(bf16[32,64,256]{2,1,0:T(8,128)(2,1)} %bitcast.13), calls=%async_computation.4 | async-start | bytes 2097152 | tf_op jit(solution)/shard_map/all_to_all | solution.py:202
  146.3 1.0 copy-start.2

commit v4 on v3

--- a/solution.py
+++ b/solution.py
@@ -10,7 +10,7 @@
 
 DH = 16
 TILE = 512
-CHUNKS = 3
+SHARES = (5, 4, 3)
 F32 = jnp.float32
 BF16 = jnp.bfloat16
 HIGHEST = lax.Precision.HIGHEST
@@ -180,32 +180,35 @@
     heads = own_heads * groups
     slices = partition_projection.shape[1]
     columns = heads * slices
-    chunk_pair = per_pair // CHUNKS
-    chunk_rows = chunk_pair * devices
-    tile = math.gcd(TILE, chunk_rows)
+    unit = per_pair // sum(SHARES)
+    ends = [unit * sum(SHARES[: at + 1]) for at in range(len(SHARES))]
+    spans = list(zip([0] + ends[:-1], ends))
+    tile = math.gcd(TILE, *(high * devices for high in ends))
 
     dest_block = inference_placement // local_rows
     target = dest_block % groups * shards + dest_block // groups
     send_key = target * local_rows + inference_placement % local_rows
     counting = jnp.arange(local_rows, dtype=jnp.int32)
     send_key, ordering = lax.sort((send_key, counting), num_keys=1)
-    ordering = ordering.reshape(devices, CHUNKS, chunk_pair)
+    ordering = ordering.reshape(devices, per_pair)
     spots = (send_key % local_rows).astype(F32).reshape(devices, per_pair)
     small = jnp.concatenate(
         [spots, jnp.broadcast_to(softmax_sharpness, (devices, own_heads))], axis=1
     )
 
     def gathered(order):
-        return layer_inputs_trainorder[order.reshape(chunk_rows)]
+        return layer_inputs_trainorder[order.reshape(-1)]
 
     def exchange(rows):
         return lax.all_to_all(rows, both, split_axis=0, concat_axis=0, tiled=True)
 
-    arrived = [exchange(gathered(ordering[:, 0]))]
+    arrived = [exchange(gathered(ordering[:, : ends[0]]))]
     small = exchange(small)
     sharpness = small.reshape(groups, shards, -1)[:, 0, per_pair:].reshape(1, heads)
-    arrived_spots = small[:, :per_pair].astype(jnp.int32).reshape(devices, CHUNKS, chunk_pair)
-    arrived_spots = arrived_spots.transpose(1, 0, 2).reshape(local_rows)
+    arrived_spots = small[:, :per_pair].astype(jnp.int32)
+    arrived_spots = jnp.concatenate(
+        [arrived_spots[:, low:high].reshape(-1) for low, high in spans]
+    )
     _, placed = lax.sort((arrived_spots, counting), num_keys=1)
 
     gain = initial_layernorm_gain[None]
@@ -236,13 +239,13 @@
     )(layer_inputs_trainorder, *operands)
 
     waiting, sums, arrived[0] = lax.optimization_barrier(
-        (gathered(ordering[:, 1]), sums, arrived[0])
+        (gathered(ordering[:, ends[0] : ends[1]]), sums, arrived[0])
     )
     part = jnp.sum(exchange(sums.reshape(devices, -1)), axis=0)
     sums = exchange(jnp.broadcast_to(part, (devices,) + part.shape)).reshape(sums.shape)
-    waiting, later, sums = lax.optimization_barrier((waiting, ordering[:, 2:], sums))
+    waiting, later, sums = lax.optimization_barrier((waiting, ordering, sums))
     arrived.append(exchange(waiting))
-    later = [gathered(later[:, at]) for at in range(CHUNKS - 2)]
+    later = [gathered(later[:, low:high]) for low, high in spans[2:]]
 
     maps = (sums, partition_question_map, partition_lookup_map, partition_content_map)
     blend = pl.pallas_call(
@@ -261,15 +264,16 @@
         perceptron_exit_offset[None],
     )
     result = ()
-    steps = chunk_rows // tile
-    for at in range(CHUNKS):
+    for at, (low, high) in enumerate(spans):
+        chunk_rows = (high - low) * devices
+        first = low * devices // tile
         result = pl.pallas_call(
             functools.partial(rows_kernel, slices),
-            grid=(steps,),
+            grid=(chunk_rows // tile,),
             in_specs=[pl.BlockSpec((tile, width), lambda i: (i, 0))]
             + [whole(a) for a in operands]
             + [pl.BlockSpec(memory_space=pl.ANY) for _ in result],
-            out_specs=(pl.BlockSpec((tile, width), lambda i, at=at: (i + at * steps, 0)),),
+            out_specs=(pl.BlockSpec((tile, width), lambda i, first=first: (i + first, 0)),),
             out_shape=(jax.ShapeDtypeStruct((local_rows, width), BF16),),
             input_output_aliases={1 + len(operands): 0} if result else {},
             compiler_params=pltpu.CompilerParams(dimension_semantics=("arbitrary",)),
@@ -278,7 +282,7 @@
                 transcendentals=chunk_rows * columns * 4,
             ),
         )(arrived[at], *operands, *result)
-        if at + 2 < CHUNKS:
+        if at + 2 < len(SHARES):
             leaving, result = lax.optimization_barrier((later[at], result))
             arrived.append(exchange(leaving))
     return result[0][placed][None]

time: 186 us -> 175 us (0.941)
  local copies, waits for them, and re-layouts: 60.6 us -> 54.9 us
  blocking collectives: 21.9 us -> 19.8 us
  starting transfers between devices: 22.2 us -> 20.2 us
    gather x3, local copies, waits for them, and re-layouts: 29 us -> 23.6 us  [gathered(): return layer_inputs_trainorder[order.reshape(-1)]]
    all_to_all x2, blocking collectives: 21.9 us -> 19.8 us  [exchange(): return lax.all_to_all(rows, both, split_axis=0, concat_axis=0, tiled=True)]
    all_to_all x4, starting transfers between devices: 22.2 us -> 20.2 us  [exchange(): return lax.all_to_all(rows, both, split_axis=0, concat_axis=0, tiled=True)]
  transfers between devices with their start and end apart: 4 -> 4, of which waited for: 2 -> 3; matrix products, arithmetic and copies ran while one was open for 21% -> 18% of each run, Pallas kernels for 25% -> 28%
where the time goes in v4:
time: 175 us
  Pallas kernels  57.8 us (33%)
  local copies, waits for them, and re-layouts  54.9 us (31%)
  starting transfers between devices  20.2 us (12%)
  blocking collectives  19.8 us (11%)
  other arithmetic  14 us (8%)
  waiting for transfers between devices  7.71 us (4%)
    pallas_call x3, Pallas kernels, body(): pl.pallas_call(functools.partial(rows_kernel, slices), grid=(chunk_rows /...  35.7 us
    gather x1, local copies, waits for them, and re-layouts, body(): return result[0][placed][None]  25.8 us
    gather x3, local copies, waits for them, and re-layouts, gathered(): return layer_inputs_trainorder[order.reshape(-1)]  23.6 us
    all_to_all x4, starting transfers between devices, exchange(): return lax.all_to_all(rows, both, split_axis=0, concat_axis=0, tiled=True)  20.2 us
    all_to_all x2, blocking collectives, exchange(): return lax.all_to_all(rows, both, split_axis=0, concat_axis=0, tiled=True)  19.8 us
    pallas_call x1, Pallas kernels, body(): pl.pallas_call(functools.partial(sums_kernel, slices), grid=(local_rows /...  18.6 us
    all_to_all x4, waiting for transfers between devices, exchange(): return lax.all_to_all(rows, both, split_axis=0, concat_axis=0, tiled=True)  7.71 us
    sort x1, other arithmetic, body(): _, placed = lax.sort((arrived_spots, counting), num_keys=1)  6.72 us
  transfers between devices with their start and end apart: 4, of which 3 were waited for; matrix products, arithmetic and copies ran while one was open for 18% of the time, Pallas kernels for 28%

profile of v4, /device:TPU:0, one launch (start us, length us, event | category | flops | bytes accessed | tf_op | source)
XLA Modules:
  0.0 174.6 jit_solution(1362965709390596040)
XLA Ops:
  0.0 0.8 fusion.3
  0.8 6.2 %sort.30 = (s32[6144]{0:T(1024)S(1)}, s32[6144]{0:T(1024)S(1)}) sort(s32[6144]{0:T(1024)S(1)} %fusion.3, s32[6144]{0:T(1024)S(1)} %iota.5), dimensions={0}, to_apply=%region_0.1 | sort | flops 79872 | bytes 98304 | tf_op jit(solution)/shard_map/sort | solution.py:192
  7.1 0.7 pad.4.clone
  7.9 0.6 all_to_all.40
  8.5 7.3 %all-to-all-start = ((f32[32,1,196]{2,1,0:T(1,128)}), f32[32,1,196]{2,1,0:T(1,128)S(1)}, u32[]{:S(2)}, u32[]{:S(2)}) async-start(f32[32,1,196]{2,1,0:T(1,128)} %all_to_all.40), calls=%async_computation | async-start | bytes 65536 | tf_op jit(solution)/shard_map/all_to_all | solution.py:203
  15.9 0.1 reshape.136
  16.1 9.3 %gather_fusion.1 = bf16[2560,256]{1,0:T(8,128)(2,1)} fusion(bf16[6144,256]{1,0:T(8,128)(2,1)} %x_ref.1, s32[3072]{0:T(1024)S(1)} %pad_clamp_fusion), kind=kCustom, calls=%fused_computation.1 | custom fusion | bytes 2631680 | tf_op jit(solution)/shard_map/gather | solution.py:200
  25.3 5.9 %all-to-all-start.1 = ((bf16[32,80,256]{2,1,0:T(8,128)(2,1)}), bf16[32,80,256]{2,1,0:T(8,128)(2,1)}, u32[]{:S(2)}, u32[]{:S(2)}) async-start(bf16[32,80,256]{2,1,0:T(8,128)(2,1)} %bitcast.21), calls=%async_computation.1 | async-start | bytes 2621440 | tf_op jit(solution)/shard_map/all_to_all | solution.py:203
  31.3 0.1 reshape.133
  31.5 9.0 %gather_fusion = bf16[2048,256]{1,0:T(8,128)(2,1)} fusion(bf16[6144,256]{1,0:T(8,128)(2,1)S(1)} %copy-done, s32[2048]{0:T(1024)S(1)} %broadcast_clamp_fusion), kind=kCustom, calls=%fused_computation | custom fusion | bytes 2105344 | tf_op jit(solution)/shard_map/gather | solution.py:200
  40.4 0.1 slice_reduce_fusion
  40.5 0.6 reshape_squeeze.3.sharp_row_ref
  41.2 18.6 %shard_map.190 = (f32[24,512]{1,0:T(8,128)}, bf16[512,256]{1,0:T(8,128)(2,1)}, bf16[512,256]{1,0:T(8,128)(2,1)}, f32[512,1]{1,0:T(8,128)}, f32[512,1]{1,0:T(8,128)}) custom-call(bf16[6144,256]{1,0:T(8,128)(2,1)} %x_ref.1, f32[1,256]{1,0:T(1,128)} %bitcast.30, f32[1,256]{1,0:T(1,128)} %bitcast.34, bf16[256,256]{1,0:T(8,128)(2,1)} %attribute_ref.1, ...), custom_call_target="tpu_custom_call" | custom-call | flops 6442450944 | bytes 25165824 | tf_op jit(solution)/shard_map/pallas_call | solution.py:227
  59.8 3.4 %all-to-all-done.1 = bf16[32,80,256]{2,1,0:T(8,128)(2,1)} async-done(((bf16[32,80,256]{2,1,0:T(8,128)(2,1)}), bf16[32,80,256]{2,1,0:T(8,128)(2,1)}, u32[]{:S(2)}, u32[]{:S(2)}) %all-to-all-start.1) | async-done | bytes 1310752 | tf_op jit(solution)/shard_map/all_to_all | solution.py:203
  63.2 0.9 all_to_all.55
  64.1 10.7 %all_to_all.62 = f32[32,1,384]{2,1,0:T(1,128)S(1)} all-to-all(f32[32,1,384]{2,1,0:T(1,128)S(1)} %all_to_all.55), channel_id=1, replica_groups=mesh['head'=4,'pts'=8] {'head','pts'}, dimensions={0} | all-to-all | bytes 98304 | tf_op jit(solution)/shard_map/all_to_all | solution.py:203
  74.9 9.0 %all_to_all.63 = f32[32,1,384]{2,1,0:T(1,128)S(1)} all-to-all(f32[32,1,384]{2,1,0:T(1,128)S(1)} %broadcast_in_dim.43), channel_id=1, replica_groups=mesh['head'=4,'pts'=8] {'head','pts'}, dimensions={0} | all-to-all | bytes 98304 | tf_op jit(solution)/shard_map/all_to_all | solution.py:203
  83.9 0.1 reduce.3
  84.0 0.6 reshape.137.sums_ref
  84.7 3.4 %all-to-all-start.5 = ((bf16[32,64,256]{2,1,0:T(8,128)(2,1)}), bf16[32,64,256]{2,1,0:T(8,128)(2,1)}, u32[]{:S(2)}, u32[]{:S(2)}) async-start(bf16[32,64,256]{2,1,0:T(8,128)(2,1)} %bitcast.22), calls=%async_computation.5 | async-start | bytes 2097152 | tf_op jit(solution)/shard_map/all_to_all | solution.py:203
  88.1 0.1 reshape.138
  88.3 5.4 %gather_fusion.2 = bf16[1536,256]{1,0:T(8,128)(2,1)} fusion(bf16[6144,256]{1,0:T(8,128)(2,1)S(1)} %copy-done.1, s32[2048]{0:T(1024)S(1)} %pad_clamp_fusion.1), kind=kCustom, calls=%fused_computation.2 | custom fusion | bytes 1579008 | tf_op jit(solution)/shard_map/gather | solution.py:200
  93.6 3.5 %shard_map.191.blend = bf16[256,512]{1,0:T(8,128)(2,1)} custom-call(f32[24,512]{1,0:T(8,128)} %reshape.137.sums_ref, f32[16,16]{1,0:T(8,128)} %question_ref.1, f32[16,16]{1,0:T(8,128)} %lookup_ref.1, f32[16,16]{1,0:T(8,128)} %content_ref.1), custom_call_target="tpu_custom_call" | custom-call | flops 262144000 | bytes 1048576 | tf_op jit(solution)/shard_map/pallas_call | solution.py:251
  97.1 14.2 %shard_map.192.earlier_and_out_0_ = bf16[6144,256]{1,0:T(8,128)(2,1)} custom-call(bf16[2560,256]{1,0:T(8,128)(2,1)} %bitcast.5.x_ref, bf16[256,512]{1,0:T(8,128)(2,1)} %shard_map.191.blend, f32[1,256]{1,0:T(1,128)} %bitcast.31, f32[1,256]{1,0:T(1,128)} %bitcast.35, bf16[512,256]{1,0:T(8,128)(2,1)} %get-tuple-element.29.w_ref, ...), custom_call_target="tpu_custom_call" | custom-call | flops 5368709120 | bytes 10485760 | tf_op jit(solution)/shard_map/pallas_call | solution.py:270
  111.4 2.8 %all-to-all-done.5 = bf16[32,64,256]{2,1,0:T(8,128)(2,1)} async-done(((bf16[32,64,256]{2,1,0:T(8,128)(2,1)}), bf16[32,64,256]{2,1,0:T(8,128)(2,1)}, u32[]{:S(2)}, u32[]{:S(2)}) %all-to-all-start.5) | async-done | bytes 1048608 | tf_op jit(solution)/shard_map/all_to_all | solution.py:203
  114.2 3.5 %all-to-all-start.4 = ((bf16[32,48,256]{2,1,0:T(8,128)(2,1)}), bf16[32,48,256]{2,1,0:T(8,128)(2,1)S(1)}, u32[]{:S(2)}, u32[]{:S(2)}) async-start(bf16[32,48,256]{2,1,0:T(8,128)(2,1)} %bitcast.11), calls=%async_computation.4 | async-start | bytes 1572864 | tf_op jit(solution)/shard_map/all_to_all | solution.py:203
  118.2 6.7 %sort.31 = (s32[6144]{0:T(1024)}, s32[6144]{0:T(1024)S(1)}) sort(s32[6144]{0:T(1024)S(1)} %pad_add_fusion, s32[6144]{0:T(1024)S(1)} %iota.6), dimensions={0}, to_apply=%region_2.3 | sort | flops 79872 | bytes 98304 | tf_op jit(solution)/shard_map/sort | solution.py:212
  124.9 11.9 %shard_map.193.earlier_and_out_0_ = bf16[6144,256]{1,0:T(8,128)(2,1)} custom-call(bf16[2048,256]{1,0:T(8,128)(2,1)} %bitcast.14.x_ref, bf16[256,512]{1,0:T(8,128)(2,1)} %shard_map.191.blend, f32[1,256]{1,0:T(1,128)} %bitcast.32, f32[1,256]{1,0:T(1,128)} %bitcast.36, bf16[512,256]{1,0:T(8,128)(2,1)} %get-tuple-element.29.w_ref, ...), custom_call_target="tpu_custom_call", output_to_operand_aliasing={{}: (16, {})} | custom-call | flops 4294967296 | bytes 8388608 | tf_op jit(solution)/shard_map/pallas_call | solution.py:270
  136.9 1.5 all-to-all-done.4
  138.4 0.9 copy-done.2
  139.2 9.5 %shard_map.194 = bf16[6144,256]{1,0:T(8,128)(2,1)} custom-call(bf16[1536,256]{1,0:T(8,128)(2,1)} %bitcast.23, bf16[256,512]{1,0:T(8,128)(2,1)} %shard_map.191.blend, f32[1,256]{1,0:T(1,128)} %bitcast.33, f32[1,256]{1,0:T(1,128)} %bitcast.37, bf16[512,256]{1,0:T(8,128)(2,1)} %get-tuple-element.29.w_ref, ...), custom_call_target="tpu_custom_call", output_to_operand_aliasing={{}: (16, {})} | custom-call | flops 3221225472 | bytes 6291456 | tf_op jit(solution)/shard_map/pallas_call | solution.py:270
  148.8 25.8 %gather_fusion.3 = bf16[6144,256]{1,0:T(8,128)(2,1)} fusion(bf16[6144,256]{1,0:T(8,128)(2,1)} %shard_map.194, s32[6144]{0:T(1024)S(1)} %fusion.5), kind=kCustom, calls=%fused_computation.3 | custom fusion | bytes 6316032 | tf_op jit(solution)/shard_map/gather | solution.py:288
  (33 shorter events, 0.9 us)
Async XLA Ops:
  8.5 16.8 %all-to-all-start = ((f32[32,1,196]{2,1,0:T(1,128)}), f32[32,1,196]{2,1,0:T(1,128)S(1)}, u32[]{:S(2)}, u32[]{:S(2)}) async-start(f32[32,1,196]{2,1,0:T(1,128)} %all_to_all.40), calls=%async_computation | async-start | bytes 65536 | tf_op jit(solution)/shard_map/all_to_all | solution.py:203
  16.0 15.4 %copy-start = (bf16[6144,256]{1,0:T(8,128)(2,1)S(1)}, bf16[6144,256]{1,0:T(8,128)(2,1)}, u32[]{:S(2)}) copy-start(bf16[6144,256]{1,0:T(8,128)(2,1)} %x_ref.1) | copy-start | bytes 9437188
  25.3 37.9 %all-to-all-start.1 = ((bf16[32,80,256]{2,1,0:T(8,128)(2,1)}), bf16[32,80,256]{2,1,0:T(8,128)(2,1)}, u32[]{:S(2)}, u32[]{:S(2)}) async-start(bf16[32,80,256]{2,1,0:T(8,128)(2,1)} %bitcast.21), calls=%async_computation.1 | async-start | bytes 2621440 | tf_op jit(solution)/shard_map/all_to_all | solution.py:203
  41.2 47.1 %copy-start.1 = (bf16[6144,256]{1,0:T(8,128)(2,1)S(1)}, bf16[6144,256]{1,0:T(8,128)(2,1)}, u32[]{:S(2)}) copy-start(bf16[6144,256]{1,0:T(8,128)(2,1)} %x_ref.1) | copy-start | bytes 9437188
  84.7 29.6 %all-to-all-start.5 = ((bf16[32,64,256]{2,1,0:T(8,128)(2,1)}), bf16[32,64,256]{2,1,0:T(8,128)(2,1)}, u32[]{:S(2)}, u32[]{:S(2)}) async-start(bf16[32,64,256]{2,1,0:T(8,128)(2,1)} %bitcast.22), calls=%async_computation.5 | async-start | bytes 2097152 | tf_op jit(solution)/shard_map/all_to_all | solution.py:203
  114.2 24.1 %all-to-all-start.4 = ((bf16[32,48,256]{2,1,0:T(8,128)(2,1)}), bf16[32,48,256]{2,1,0:T(8,128)(2,1)S(1)}, u32[]{:S(2)}, u32[]{:S(2)}) async-start(bf16[32,48,256]{2,1,0:T(8,128)(2,1)} %bitcast.11), calls=%async_computation.4 | async-start | bytes 1572864 | tf_op jit(solution)/shard_map/all_to_all | solution.py:203
  138.4 0.9 copy-start.2
